TPU v7x, 128 devices: a whole 4x4x4 slice. The times are simulated.
128 devices in a mesh: blk: 32 (over x, y_hi, z), span: 4 (over y_lo, core).
Axes of the slice: x: 4, y: 4 (y_hi: 2, y_lo: 2; y = y_hi * 2 + y_lo), z: 4, core: 2. Of those that a mesh axis runs over, the one named last changes fastest.
Arguments:
- fields: float32 [5, 125, 65536], P(None, None, ('blk', 'span')), may hold values from -6 to 6
- section_store: float32 [5, 125, 65536], P(None, None, ('blk', 'span')), may hold values from -6 to 6
- mean_velocity: float32 [3, 125, 65536], P(None, None, ('blk', 'span')), may hold values from -0.6 to 0.6
- sound_speed: float32 [125, 65536], P(None, ('blk', 'span')), may hold values from 0.7 to 1.5
- element_slot: int32 [65536], P(('blk', 'span')), may hold values from 0 to 511, as said below
- face_turn: int32 [32, 16], P('blk', 'span'), may hold values from 0 to 7
- rotor_offset: int32 [16], P('span'), may hold values from 0 to 31
Outputs:
- fields_next: float32 [5, 125, 65536], P(None, None, ('blk', 'span'))
- store_next: float32 [5, 125, 65536], P(None, None, ('blk', 'span'))
Inputs may be any that keep to these rules, and one draw needn't show every extreme that they name: `element_slot`: in each aligned block of 512 entries (the elements of one device) every number 0 to 511 appears once.
All inputs are finite; a program needn't handle non-finite values.
Results may differ from a plain program's by a relative error of at most 0.0003.
Values sent between devices are 32-bit elements; how exact they have to be, the bound alone decides.
A program may use at most 128 MiB of HBM per device.

v0:
```python
import functools

import jax
import jax.numpy as jnp
import numpy as np
from jax import lax
from jax.experimental import pallas as pl
from jax.experimental.pallas import tpu as pltpu
from jax.sharding import PartitionSpec as P

MESH = pl.DeviceIdType.MESH
F32, BF16, I32 = jnp.float32, jnp.bfloat16, jnp.int32

section_decay = -567301805773.0 / 1357537059087.0
section_gain = 5161836677717.0 / 13612068292357.0
time_step = 0.05
metric_scale = (1.0, 1.5, 0.75)
end_weight = 0.1

NB = 512
HALF = 64
RADICES = (4, 2, 4)
CHUNKS = ((0, 48), (48, 48), (96, 48), (144, 32))
PACK_ROWS = 176


def lobatto_slopes():
    root = np.sqrt(3.0 / 7.0)
    x = np.array([-1.0, -root, 0.0, root, 1.0])
    table = np.zeros((5, 5))
    for r in range(5):
        for c in range(5):
            others = [o for o in range(5) if o != r]
            if r == c:
                table[r, c] = sum(1.0 / (x[r] - x[o]) for o in others)
            else:
                top = np.prod([x[r] - x[o] for o in others])
                low = np.prod([x[c] - x[o] for o in range(5) if o != c])
                table[r, c] = top / (low * (x[r] - x[c]))
    return table


def slope_matrices():
    d, e = lobatto_slopes(), np.eye(5)
    full = [np.kron(np.kron(d, e), e), np.kron(np.kron(e, d), e), np.kron(np.kron(e, e), d)]
    return np.stack([-g * m for g, m in zip(metric_scale, full)]).astype(np.float32)


def halves(x):
    high = x.astype(BF16)
    return high, (x - high.astype(F32)).astype(BF16)


def moved(x, table, transposed=False):
    rows = x.shape[0]
    high, low = halves(x)
    both = jnp.concatenate([high, low], axis=0)
    dims = (((1,), (1 if transposed else 0,)), ((), ()))
    out = lax.dot_general(both, table, dims, preferred_element_type=F32)
    return out[:rows] + out[rows:]


def flux(q, m, c, d):
    out = [m * v for v in q]
    out[0] = out[0] + c * q[1 + d]
    out[1 + d] = out[1 + d] + c * q[4]
    out[4] = out[4] + c * q[1 + d]
    return out


def face_parts(left, right, d):
    ql, ml, cl = left[:5], left[5], left[6]
    qr, mr, cr = right[:5], right[5], right[6]
    reach = jnp.maximum(jnp.abs(ml) + cl, jnp.abs(mr) + cr)
    fl, fr = flux(ql, ml, cl, d), flux(qr, mr, cr, d)
    return [a - b for a, b in zip(fl, fr)], [reach * (b - a) for a, b in zip(ql, qr)]


def one_hot(row, count):
    k = lax.broadcasted_iota(I32, (count, row.shape[1]), 0).astype(F32)
    return jnp.where(k == row, 1.0, 0.0).astype(BF16)


def turned(x, code, inverse):
    lane = lax.broadcasted_iota(I32, (8, 128), 1)
    n = lane & 31
    i = (n * 13) >> 6
    k = n - i * 5
    ok = n < 25
    base = lane - n

    def apply(v, bit, target):
        index = jnp.where(ok, base + target, lane)
        return jnp.where((code & bit) != 0, jnp.take_along_axis(v, index, axis=1), v)

    swap, first, second = (4, k * 5 + i), (1, (4 - i) * 5 + k), (2, i * 5 + 4 - k)
    for bit, target in (second, first, swap) if inverse else (swap, first, second):
        x = apply(x, bit, target)
    return x


def kernel(
    radices,
    nblk,
    nspan,
    fields,
    mean,
    sound,
    slot_hbm,
    slopes_hbm,
    turn,
    offset,
    rates,
    x,
    acc,
    slot,
    slopes,
    table,
    pack,
    recv,
    near,
    face,
    grid,
    corr,
    sp_send,
    sp_recv,
    stage,
    hops,
    load_sem,
    circ_send,
    circ_recv,
    span_send,
    span_recv,
    hop_send,
    hop_recv,
):
    t = lax.axis_index("blk")
    slab = lax.axis_index("span")
    after, before = lax.rem(t + 1, nblk), lax.rem(t + nblk - 1, nblk)
    above, below = lax.rem(slab + 1, nspan), lax.rem(slab + nspan - 1, nspan)

    digits, weights, rest, weight = [], [], t, 1
    for radix in radices:
        digits.append(lax.rem(rest, radix))
        weights.append(weight)
        rest = rest // radix
        weight *= radix
    peers = []
    for pos, radix in enumerate(radices):
        for step in range(1, radix):
            to = t + (lax.rem(digits[pos] + step, radix) - digits[pos]) * weights[pos]
            peers.append((pos, step, to))

    barrier = pltpu.get_barrier_semaphore()
    for to in (after, before):
        pl.semaphore_signal(barrier, inc=1, device_id={"blk": to}, device_id_type=MESH)
    for to in (above, below):
        pl.semaphore_signal(barrier, inc=1, device_id={"span": to}, device_id_type=MESH)
    for _, _, to in peers:
        pl.semaphore_signal(barrier, inc=1, device_id={"blk": to}, device_id_type=MESH)

    def load(src):
        if src < 5:
            array = fields.at[src]
        else:
            array = mean.at[src - 5] if src < 8 else sound
        return [
            pltpu.make_async_copy(array.at[:, pl.ds(128 * b, 128)], x.at[src, b], load_sem.at[src, b])
            for b in range(4)
        ]

    def cells(src, rows=slice(0, 125)):
        return jnp.concatenate([x[src, b, rows, :] for b in range(4)], axis=1)

    load_slot = pltpu.make_async_copy(slot_hbm, slot, load_sem.at[9, 0])
    load_slopes = pltpu.make_async_copy(slopes_hbm, slopes, load_sem.at[9, 1])
    load_slot.start()
    for src in (0, 1, 2, 3, 4, 5, 8, 6, 7):
        for copy in load(src):
            copy.start()
    load_slopes.start()

    load_slot.wait()
    slot_row = slot[...].astype(F32)
    table[...] = one_hot(slot_row, NB)
    for end in range(2):
        pack[end, 0:1, :] = slot_row

    for at, src in enumerate((0, 1, 2, 3, 4, 5, 8)):
        for copy in load(src):
            copy.wait()
        for end in range(2):
            pack[end, 1 + 25 * at : 26 + 25 * at, :] = cells(src, slice(100 * end, 100 * end + 25))

    pl.semaphore_wait(barrier, 4 + len(peers))

    def circ(end, part):
        start, rows = CHUNKS[part]
        return pltpu.make_async_remote_copy(
            src_ref=pack.at[end, pl.ds(start, rows), :],
            dst_ref=recv.at[1 - end, pl.ds(start, rows), :],
            send_sem=circ_send.at[end, part],
            recv_sem=circ_recv.at[1 - end, part],
            device_id={"blk": after if end == 1 else before},
            device_id_type=MESH,
        )

    for end in range(2):
        circ(end, 0).start()

    for src in (6, 7):
        for copy in load(src):
            copy.wait()
    for d in (2, 1):
        for at, src in enumerate((0, 1, 2, 3, 4, 4 + 1 + d, 8)):
            for end in range(2):
                kind = 2 * (d - 1) + end
                if d == 2:
                    face[kind, 32 * at : 32 * at + 25, :] = cells(src, pl.ds(4 * end, 25, stride=5))
                else:
                    for i in range(5):
                        rows = slice(25 * i + 20 * end, 25 * i + 20 * end + 5)
                        face[kind, 32 * at + 5 * i : 32 * at + 5 * i + 5, :] = cells(src, rows)

    lane = lax.broadcasted_iota(I32, (8, NB), 1)
    sub = lax.broadcasted_iota(I32, (8, NB), 0)
    wanted = jnp.where(sub < 4, sub * 128 + (HALF - 1), (sub - 4) * 128 + HALF)
    column = jnp.sum(jnp.where(lane == wanted, slot_row, 0.0), axis=1, keepdims=True)
    hot = jnp.where(lane.astype(F32) == column, 1.0, 0.0)
    dims = (((1,), (1,)), ((), ()))
    packet = jnp.zeros((8, 256), F32)
    for kind, rows in ((3, sub < 4), (2, sub >= 4)):
        pick = jnp.where(rows, hot, 0.0).astype(BF16)
        for part in halves(face[kind]):
            packet = packet + lax.dot_general(pick, part, dims, preferred_element_type=F32)

    sub1 = lax.broadcasted_iota(I32, (8, 128), 0)
    row = sub1 & 3
    is_stator = sub1 < 4

    def per_row(values):
        out = jnp.full((8, 128), values[3], I32)
        for s in range(3):
            out = jnp.where(row == s, values[s], out)
        return out

    code = per_row([turn[0, s] for s in range(4)])
    shift = per_row([offset[s] for s in range(4)])
    shift = jnp.where(is_stator, shift, (nblk - shift) & (nblk - 1))
    pair = [packet[:, :128], packet[:, 128:]]
    pair = [jnp.where(is_stator, p, turned(p, code, True)) for p in pair]

    def hop(number):
        pos, step, to = peers[number]
        return pltpu.make_async_remote_copy(
            src_ref=stage.at[pos],
            dst_ref=hops.at[number],
            send_sem=hop_send.at[number],
            recv_sem=hop_recv.at[number],
            device_id={"blk": to},
            device_id_type=MESH,
        )

    def start_hops(pos, pair):
        for h in range(2):
            stage[pos, :, 128 * h : 128 * h + 128] = pair[h]
        for number, (p, _, _) in enumerate(peers):
            if p == pos:
                hop(number).start()

    start_hops(0, pair)
    for part in range(1, len(CHUNKS)):
        for end in range(2):
            circ(end, part).start()

    for kind in (1, 0):
        grid[kind] = moved(face[kind], table[...])
        sp_send[kind] = grid[kind, 0:224, 384 * kind : 384 * kind + 128]

    def span(end):
        return pltpu.make_async_remote_copy(
            src_ref=sp_send.at[end],
            dst_ref=sp_recv.at[1 - end],
            send_sem=span_send.at[end],
            recv_sem=span_recv.at[1 - end],
            device_id={"span": above if end == 1 else below},
            device_id_type=MESH,
        )

    for end in range(2):
        span(end).start()
    for kind in (2, 3):
        grid[kind] = moved(face[kind], table[...])

    carry = jnp.zeros((8, 128), I32)

    def take_hops(pos, pair, carry):
        radix = radices[pos]
        digit = lax.rem(shift // weights[pos], radix) + carry
        source = lax.rem(digits[pos] + 2 * radix - digit, radix)
        next_carry = (source + digit - digits[pos]) // radix
        distance = lax.rem(digit, radix)
        for number, (p, step, _) in enumerate(peers):
            if p == pos:
                hop(number).wait()
                for h in range(2):
                    arrived = hops[number, :, 128 * h : 128 * h + 128]
                    pair[h] = jnp.where(distance == step, arrived, pair[h])
        return pair, next_carry

    load_slopes.wait()
    velocity = (5, 6, 7)

    def volume(f):
        total = None
        for d in range(3):
            fx = cells(velocity[d]) * cells(f)
            if f == 0 or f == 4:
                fx = fx + cells(8) * cells(1 + d)
            elif f == 1 + d:
                fx = fx + cells(8) * cells(4)
            part = jnp.dot(slopes[d], fx, precision=lax.Precision.HIGHEST, preferred_element_type=F32)
            total = part if total is None else total + part
        for b in range(4):
            acc[f, b] = total[:, 128 * b : 128 * b + 128]

    todo = [[0, 1], [2, 3], [4]]
    for pos in range(len(radices)):
        for f in todo[pos] if pos < 3 else []:
            volume(f)
        pair, carry = take_hops(pos, pair, carry)
        if pos + 1 < len(radices):
            start_hops(pos + 1, pair)
    for later in todo[len(radices) :]:
        for f in later:
            volume(f)

    pair = [jnp.where(is_stator, turned(p, code, False), p) for p in pair]
    arrived = jnp.concatenate(pair, axis=1)
    put = jnp.where(lane == jnp.where(sub < 4, sub * 128 + HALF, (sub - 4) * 128 + HALF - 1), 1.0, 0.0)
    first = jnp.where(sub < 4, put, 0.0), jnp.where(sub >= 4, put, 0.0)
    tn = (((0,), (0,)), ((), ()))
    spread = [
        lax.dot_general(arrived, p, tn, precision=lax.Precision.HIGHEST, preferred_element_type=F32)
        for p in first
    ]

    for end in range(2):
        span(end).wait()
    w = 0.5 * metric_scale[1] / end_weight
    for b in range(5):
        left, right = [], []
        for f in range(7):
            rows = slice(32 * f, 32 * f + 32)
            if b > 0:
                left.append(grid[1, rows, 128 * b - 128 : 128 * b])
            if b < 4:
                right.append(grid[0, rows, 128 * b : 128 * b + 128])
        for f in range(7):
            rows = slice(32 * f, 32 * f + 32)
            if b == 0:
                wall = -right[f] if f == 2 else right[f]
                left.append(jnp.where(slab > 0, sp_recv[0, rows, :], wall))
            if b == 4:
                wall = -left[f] if f == 2 else left[f]
                right.append(jnp.where(slab < nspan - 1, sp_recv[1, rows, :], wall))
        diff, jump = face_parts(left, right, 1)
        for f in range(5):
            if b > 0:
                corr[1, 32 * f : 32 * f + 32, 128 * b - 128 : 128 * b] = w * (diff[f] + jump[f])
            if b < 4:
                corr[0, 32 * f : 32 * f + 32, 128 * b : 128 * b + 128] = w * (diff[f] - jump[f])

    w = 0.5 * metric_scale[2] / end_weight
    axial = lax.broadcasted_iota(I32, (32, 128), 1)
    for s in range(4):
        cols = slice(128 * s, 128 * s + 128)
        low = [grid[2, 32 * f : 32 * f + 32, cols] for f in range(7)]
        high = [grid[3, 32 * f : 32 * f + 32, cols] for f in range(7)]
        for end in range(2):
            own, far = (high, low) if end else (low, high)
            outer = []
            for f in range(7):
                v = pltpu.roll(far[f], 127 if end else 1, axis=1)
                v = jnp.where(
                    axial == (HALF - 1 if end else HALF), spread[end][32 * f : 32 * f + 32, cols], v
                )
                edge = own[f] if f >= 5 else 0.0
                outer.append(jnp.where(axial == (127 if end else 0), edge, v))
            diff, jump = face_parts(own if end else outer, outer if end else own, 2)
            for f in range(5):
                value = diff[f] + jump[f] if end else diff[f] - jump[f]
                corr[2 + end, 32 * f : 32 * f + 32, cols] = w * value

    for kind in range(4):
        back = moved(corr[kind], table[...], transposed=True)
        grid[kind, 0:160, :] = back
    for f in range(5):
        for end in range(2):
            for i in range(5):
                rows = slice(25 * i + 20 * end, 25 * i + 20 * end + 5)
                for b in range(4):
                    cols = slice(128 * b, 128 * b + 128)
                    acc[f, b, rows, :] += grid[end, 32 * f + 5 * i : 32 * f + 5 * i + 5, cols]
            lines = pl.ds(4 * end, 25, stride=5)
            for b in range(4):
                cols = slice(128 * b, 128 * b + 128)
                acc[f, b, lines, :] = acc[f, b, lines, :] + grid[2 + end, 32 * f : 32 * f + 25, cols]

    w = 0.5 * metric_scale[0] / end_weight
    for end in range(2):
        for part in range(len(CHUNKS)):
            circ(1 - end, part).wait_recv()
            if part == 0:
                other = one_hot(recv[end, 0:1, :], NB)
                swap = lax.dot_general(other, table[...], dims, preferred_element_type=F32).astype(BF16)
        near[end] = moved(recv[end], swap)
        rows = slice(100 * end, 100 * end + 25)
        own = [cells(src, rows) for src in (0, 1, 2, 3, 4, 5, 8)]
        outer = [near[end, 1 + 25 * f : 26 + 25 * f, :] for f in range(7)]
        diff, jump = face_parts(own if end else outer, outer if end else own, 0)
        for f in range(5):
            value = diff[f] + jump[f] if end else diff[f] - jump[f]
            for b in range(4):
                acc[f, b, rows, :] += w * value[:, 128 * b : 128 * b + 128]
    for end in range(2):
        for part in range(len(CHUNKS)):
            circ(end, part).wait_send()
    for f in range(5):
        for b in range(4):
            rates[f, :, 128 * b : 128 * b + 128] = acc[f, b]


def on_device(mesh, radices, fields, section_store, mean_velocity, sound_speed, element_slot, face_turn, rotor_offset):
    nblk, nspan = mesh.shape["blk"], mesh.shape["span"]
    hop_count = sum(r - 1 for r in radices)
    anywhere = pl.BlockSpec(memory_space=pl.ANY)
    dma = pltpu.SemaphoreType.DMA
    rates = pl.pallas_call(
        functools.partial(kernel, radices, nblk, nspan),
        out_shape=jax.ShapeDtypeStruct((5, 125, NB), F32),
        in_specs=[anywhere] * 5 + [pl.BlockSpec(memory_space=pltpu.SMEM)] * 2,
        out_specs=pl.BlockSpec(memory_space=pltpu.VMEM),
        scratch_shapes=[
            pltpu.VMEM((9, 4, 125, 128), F32),
            pltpu.VMEM((5, 4, 125, 128), F32),
            pltpu.VMEM((1, NB), I32),
            pltpu.VMEM((3, 125, 125), F32),
            pltpu.VMEM((NB, NB), BF16),
            pltpu.VMEM((2, PACK_ROWS, NB), F32),
            pltpu.VMEM((2, PACK_ROWS, NB), F32),
            pltpu.VMEM((2, PACK_ROWS, NB), F32),
            pltpu.VMEM((4, 256, NB), F32),
            pltpu.VMEM((4, 256, NB), F32),
            pltpu.VMEM((4, 160, NB), F32),
            pltpu.VMEM((2, 224, 128), F32),
            pltpu.VMEM((2, 224, 128), F32),
            pltpu.VMEM((len(radices), 8, 256), F32),
            pltpu.VMEM((hop_count, 8, 256), F32),
            dma((10, 4)),
            dma((2, len(CHUNKS))),
            dma((2, len(CHUNKS))),
            dma((2,)),
            dma((2,)),
            dma((hop_count,)),
            dma((hop_count,)),
        ],
        compiler_params=pltpu.CompilerParams(
            collective_id=0, has_side_effects=True, vmem_limit_bytes=40 * 2**20
        ),
        name="rates",
    )(
        fields,
        mean_velocity,
        sound_speed,
        element_slot.reshape(1, NB),
        jnp.asarray(slope_matrices()),
        face_turn,
        rotor_offset,
    )
    store_next = section_decay * section_store + time_step * rates
    fields_next = fields + section_gain * store_next
    return fields_next, store_next


def solution(mesh, radices=RADICES):
    both = ("blk", "span")
    in_specs = (
        P(None, None, both),
        P(None, None, both),
        P(None, None, both),
        P(None, both),
        P(both),
        P("blk", "span"),
        P("span"),
    )
    return jax.shard_map(
        functools.partial(on_device, mesh, radices),
        mesh=mesh,
        in_specs=in_specs,
        out_specs=(P(None, None, both), P(None, None, both)),
        check_vma=False,
    )
```

profile of v0, /device:TPU:24, one launch (start us, length us, event | category | flops | bytes accessed | tf_op | source)
XLA Modules:
  0.0 39.2 jit_solution(17781037442969838520)
XLA Ops:
  0.6 0.0 copy-start
  0.6 1.3 %copy-done = f32[5,125,512]{2,1,0:T(8,128)S(1)} copy-done((f32[5,125,512]{2,1,0:T(8,128)S(1)}, f32[5,125,512]{2,1,0:T(8,128)}, u32[]{:S(2)}) %copy-start) | copy-done | bytes 1280024
  1.9 0.0 copy-start.1
  2.0 1.1 %copy-done.1 = f32[3,125,512]{2,1,0:T(8,128)S(1)} copy-done((f32[3,125,512]{2,1,0:T(8,128)S(1)}, f32[3,125,512]{2,1,0:T(8,128)}, u32[]{:S(2)}) %copy-start.1) | copy-done | bytes 768024
  3.1 0.0 copy-start.2
  3.1 0.9 %copy-done.2 = f32[125,512]{1,0:T(8,128)S(1)} copy-done((f32[125,512]{1,0:T(8,128)S(1)}, f32[125,512]{1,0:T(8,128)}, u32[]{:S(2)}) %copy-start.2) | copy-done | bytes 256024
  4.0 0.0 copy-start.3
  4.0 0.9 %copy-done.3 = f32[3,125,125]{2,1,0:T(8,128)S(1)} copy-done((f32[3,125,125]{2,1,0:T(8,128)S(1)}, f32[3,125,125]{2,1,0:T(8,128)}, u32[]{:S(2)}) %copy-start.3) | copy-done | bytes 187524
  5.0 0.0 copy-start.4
  5.0 0.7 %copy-done.4 = s32[512]{0:T(512)S(1)} copy-done((s32[512]{0:T(512)S(1)}, s32[512]{0:T(512)}, u32[]{:S(2)}) %copy-start.4) | copy-done | bytes 2072
  5.6 0.0 copy-start.5
  5.6 0.7 %copy-done.5 = s32[1,4]{1,0:T(1,128)S(1)} copy-done((s32[1,4]{1,0:T(1,128)S(1)}, s32[1,4]{1,0:T(1,128)}, u32[]{:S(2)}) %copy-start.5) | copy-done | bytes 40
  6.3 0.0 copy-start.6
  6.3 0.7 %copy-done.6 = s32[4]{0:T(128)S(1)} copy-done((s32[4]{0:T(128)S(1)}, s32[4]{0:T(128)}, u32[]{:S(2)}) %copy-start.6) | copy-done | bytes 40
  7.0 0.0 copy-start.7
  7.0 30.3 %rates.1 = f32[5,125,512]{2,1,0:T(8,128)S(1)} custom-call(f32[5,125,512]{2,1,0:T(8,128)S(1)} %copy-done, f32[3,125,512]{2,1,0:T(8,128)S(1)} %copy-done.1, f32[125,512]{1,0:T(8,128)S(1)} %copy-done.2, s32[1,512]{1,0:T(1,128)S(1)} %bitcast.1, f32[3,125,125]{2,1,0:T(8,128)S(1)} %copy-done.3, s32[1,4]{1,0:T(1,128)S(1)} %copy-done.5, s32[4]{0:T(128)S(1)} %copy-done.6), custom_call_target="tpu_custom_call" | custom-call | tf_op jit(solution)/shard_map/rates/pallas_call | solution.py:439
  37.2 0.0 copy-done.7
  37.3 2.0 %multiply_add_fusion = (f32[5,125,512]{2,1,0:T(8,128)}, f32[5,125,512]{2,1,0:T(8,128)}) fusion(f32[5,125,512]{2,1,0:T(8,128)S(1)} %copy-done, f32[5,125,512]{2,1,0:T(8,128)S(1)} %rates.1, f32[5,125,512]{2,1,0:T(8,128)S(1)} %copy-done.7), kind=kLoop, calls=%fused_computation | loop fusion | flops 1600000 | bytes 6400000 | tf_op jit(solution)/shard_map/add | solution.py:482
Async XLA Ops:
  0.6 1.3 %copy-start = (f32[5,125,512]{2,1,0:T(8,128)S(1)}, f32[5,125,512]{2,1,0:T(8,128)}, u32[]{:S(2)}) copy-start(f32[5,125,512]{2,1,0:T(8,128)} %fields.1) | copy-start | bytes 3840004
  1.9 1.1 %copy-start.1 = (f32[3,125,512]{2,1,0:T(8,128)S(1)}, f32[3,125,512]{2,1,0:T(8,128)}, u32[]{:S(2)}) copy-start(f32[3,125,512]{2,1,0:T(8,128)} %mean.1) | copy-start | bytes 2304004
  3.1 0.9 %copy-start.2 = (f32[125,512]{1,0:T(8,128)S(1)}, f32[125,512]{1,0:T(8,128)}, u32[]{:S(2)}) copy-start(f32[125,512]{1,0:T(8,128)} %sound.1) | copy-start | bytes 768004
  4.0 0.9 %copy-start.3 = (f32[3,125,125]{2,1,0:T(8,128)S(1)}, f32[3,125,125]{2,1,0:T(8,128)}, u32[]{:S(2)}) copy-start(f32[3,125,125]{2,1,0:T(8,128)} %constant.8.clone.slopes_hbm) | copy-start | bytes 562504
  5.0 0.7 %copy-start.4 = (s32[512]{0:T(512)S(1)}, s32[512]{0:T(512)}, u32[]{:S(2)}) copy-start(s32[512]{0:T(512)} %param.12) | copy-start | bytes 6148
  5.6 0.7 %copy-start.5 = (s32[1,4]{1,0:T(1,128)S(1)}, s32[1,4]{1,0:T(1,128)}, u32[]{:S(2)}) copy-start(s32[1,4]{1,0:T(1,128)} %turn.1) | copy-start | bytes 52
  6.3 0.7 %copy-start.6 = (s32[4]{0:T(128)S(1)}, s32[4]{0:T(128)}, u32[]{:S(2)}) copy-start(s32[4]{0:T(128)} %offset.1) | copy-start | bytes 52
  7.0 30.3 %copy-start.7 = (f32[5,125,512]{2,1,0:T(8,128)S(1)}, f32[5,125,512]{2,1,0:T(8,128)}, u32[]{:S(2)}) copy-start(f32[5,125,512]{2,1,0:T(8,128)} %param.9) | copy-start | bytes 3840004
where the time goes:
time: 39.5 us; the launch traced here: 39.2 us
  Pallas kernels  30.3 us (77%)
  local copies, waits for them, and re-layouts  6.31 us (16%)
  other arithmetic  1.98 us (5%)
  between operations  0.66 us (2%)
    pallas_call x1, Pallas kernels, on_device(): pl.pallas_call(functools.partial(kernel, radices, nblk, nspan), out_shape...  30.3 us
    unnamed x16, local copies, waits for them, and re-layouts  6.31 us
    add x1, other arithmetic, on_device(): fields_next = fields + section_gain * store_next  1.98 us

commit v1 on v0

--- a/solution.py
+++ b/solution.py
@@ -108,9 +108,11 @@
     sound,
     slot_hbm,
     slopes_hbm,
+    turn_hbm,
+    offset_hbm,
+    rates,
     turn,
     offset,
-    rates,
     x,
     acc,
     slot,
@@ -174,11 +176,15 @@
 
     load_slot = pltpu.make_async_copy(slot_hbm, slot, load_sem.at[9, 0])
     load_slopes = pltpu.make_async_copy(slopes_hbm, slopes, load_sem.at[9, 1])
+    load_turn = pltpu.make_async_copy(turn_hbm, turn, load_sem.at[9, 2])
+    load_offset = pltpu.make_async_copy(offset_hbm, offset, load_sem.at[9, 3])
     load_slot.start()
     for src in (0, 1, 2, 3, 4, 5, 8, 6, 7):
         for copy in load(src):
             copy.start()
     load_slopes.start()
+    load_turn.start()
+    load_offset.start()
 
     load_slot.wait()
     slot_row = slot[...].astype(F32)
@@ -244,6 +250,8 @@
             out = jnp.where(row == s, values[s], out)
         return out
 
+    load_turn.wait()
+    load_offset.wait()
     code = per_row([turn[0, s] for s in range(4)])
     shift = per_row([offset[s] for s in range(4)])
     shift = jnp.where(is_stator, shift, (nblk - shift) & (nblk - 1))
@@ -434,14 +442,16 @@
 def on_device(mesh, radices, fields, section_store, mean_velocity, sound_speed, element_slot, face_turn, rotor_offset):
     nblk, nspan = mesh.shape["blk"], mesh.shape["span"]
     hop_count = sum(r - 1 for r in radices)
-    anywhere = pl.BlockSpec(memory_space=pl.ANY)
+    anywhere = pl.BlockSpec(memory_space=pltpu.HBM)
     dma = pltpu.SemaphoreType.DMA
     rates = pl.pallas_call(
         functools.partial(kernel, radices, nblk, nspan),
         out_shape=jax.ShapeDtypeStruct((5, 125, NB), F32),
-        in_specs=[anywhere] * 5 + [pl.BlockSpec(memory_space=pltpu.SMEM)] * 2,
+        in_specs=[anywhere] * 7,
         out_specs=pl.BlockSpec(memory_space=pltpu.VMEM),
         scratch_shapes=[
+            pltpu.SMEM((1, 4), I32),
+            pltpu.SMEM((4,), I32),
             pltpu.VMEM((9, 4, 125, 128), F32),
             pltpu.VMEM((5, 4, 125, 128), F32),
             pltpu.VMEM((1, NB), I32),
@@ -470,13 +480,18 @@
         ),
         name="rates",
     )(
-        fields,
-        mean_velocity,
-        sound_speed,
-        element_slot.reshape(1, NB),
-        jnp.asarray(slope_matrices()),
-        face_turn,
-        rotor_offset,
+        *[
+            pltpu.with_memory_space_constraint(value, pltpu.HBM)
+            for value in (
+                fields,
+                mean_velocity,
+                sound_speed,
+                element_slot.reshape(1, NB),
+                jnp.asarray(slope_matrices()),
+                face_turn,
+                rotor_offset,
+            )
+        ]
     )
     store_next = section_decay * section_store + time_step * rates
     fields_next = fields + section_gain * store_next

time: 39.5 us -> 32.6 us (0.83)
  the two profiles are of different devices: /device:TPU:24 before, /device:TPU:0 now
where the time goes in v1:
time: 32.6 us; the launch traced here: 32.5 us
  Pallas kernels  29.8 us (91%)
  other arithmetic  1.97 us (6%)
  between operations  0.67 us (2%)
    pallas_call x1, Pallas kernels, on_device(): pl.pallas_call(functools.partial(kernel, radices, nblk, nspan), out_shape...  29.8 us
    add x1, other arithmetic, on_device(): fields_next = fields + section_gain * store_next  1.97 us

profile of v1, /device:TPU:0, one launch (start us, length us, event | category | flops | bytes accessed | tf_op | source)
XLA Modules:
  0.0 32.5 jit_solution(15420526690926780449)
XLA Ops:
  0.6 0.0 copy-start
  0.6 0.0 copy-start.1
  0.7 29.8 %rates.1 = f32[5,125,512]{2,1,0:T(8,128)S(1)} custom-call(f32[5,125,512]{2,1,0:T(8,128)} %fields.1, f32[3,125,512]{2,1,0:T(8,128)} %mean.1, f32[125,512]{1,0:T(8,128)} %sound.1, s32[1,512]{1,0:T(1,128)} %bitcast.1, f32[3,125,125]{2,1,0:T(8,128)} %constant.8.clone.slopes_hbm, s32[1,4]{1,0:T(1,128)} %turn_hbm.1, s32[4]{0:T(128)} %offset_hbm.1), custom_call_target="tpu_custom_call" | custom-call | tf_op jit(solution)/shard_map/rates/pallas_call | solution.py:447
  30.5 0.0 copy-done
  30.5 0.0 copy-done.1
  30.5 2.0 %multiply_add_fusion = (f32[5,125,512]{2,1,0:T(8,128)}, f32[5,125,512]{2,1,0:T(8,128)}) fusion(f32[5,125,512]{2,1,0:T(8,128)S(1)} %copy-done, f32[5,125,512]{2,1,0:T(8,128)S(1)} %rates.1, f32[5,125,512]{2,1,0:T(8,128)S(1)} %copy-done.1), kind=kLoop, calls=%fused_computation | loop fusion | flops 1600000 | bytes 6400000 | tf_op jit(solution)/shard_map/add | solution.py:497
Async XLA Ops:
  0.6 29.9 %copy-start = (f32[5,125,512]{2,1,0:T(8,128)S(1)}, f32[5,125,512]{2,1,0:T(8,128)}, u32[]{:S(2)}) copy-start(f32[5,125,512]{2,1,0:T(8,128)} %fields.1) | copy-start | bytes 3840004
  0.6 29.9 %copy-start.1 = (f32[5,125,512]{2,1,0:T(8,128)S(1)}, f32[5,125,512]{2,1,0:T(8,128)}, u32[]{:S(2)}) copy-start(f32[5,125,512]{2,1,0:T(8,128)} %param.9) | copy-start | bytes 3840004

commit v2 on v1

--- a/solution.py
+++ b/solution.py
@@ -20,8 +20,9 @@
 NB = 512
 HALF = 64
 RADICES = (4, 2, 4)
-CHUNKS = ((0, 48), (48, 48), (96, 48), (144, 32))
+CHUNKS = ((0, 32), (32, 64), (96, 56), (152, 24))
 PACK_ROWS = 176
+PACK_ORDER = (5, 8, 1, 4, 0, 2, 3)
 
 
 def lobatto_slopes():
@@ -43,7 +44,9 @@
 def slope_matrices():
     d, e = lobatto_slopes(), np.eye(5)
     full = [np.kron(np.kron(d, e), e), np.kron(np.kron(e, d), e), np.kron(np.kron(e, e), d)]
-    return np.stack([-g * m for g, m in zip(metric_scale, full)]).astype(np.float32)
+    full = np.stack([-g * m for g, m in zip(metric_scale, full)])
+    high = full.astype(BF16)
+    return np.stack([high, (full - high.astype(np.float64)).astype(BF16)])
 
 
 def halves(x):
@@ -60,20 +63,25 @@
     return out[:rows] + out[rows:]
 
 
-def flux(q, m, c, d):
-    out = [m * v for v in q]
-    out[0] = out[0] + c * q[1 + d]
-    out[1 + d] = out[1 + d] + c * q[4]
-    out[4] = out[4] + c * q[1 + d]
-    return out
+def reach_of(left, right):
+    return jnp.maximum(jnp.abs(left[5]) + left[6], jnp.abs(right[5]) + right[6])
+
+
+def face_value(left, right, d, reach, f):
+    sides = []
+    for q in (left, right):
+        flux = q[5] * q[f]
+        if f == 0 or f == 4:
+            flux = flux + q[6] * q[1 + d]
+        elif f == 1 + d:
+            flux = flux + q[6] * q[4]
+        sides.append(flux)
+    return sides[0] - sides[1], reach * (right[f] - left[f])
 
 
 def face_parts(left, right, d):
-    ql, ml, cl = left[:5], left[5], left[6]
-    qr, mr, cr = right[:5], right[5], right[6]
-    reach = jnp.maximum(jnp.abs(ml) + cl, jnp.abs(mr) + cr)
-    fl, fr = flux(ql, ml, cl, d), flux(qr, mr, cr, d)
-    return [a - b for a, b in zip(fl, fr)], [reach * (b - a) for a, b in zip(ql, qr)]
+    reach = reach_of(left, right)
+    return zip(*[face_value(left, right, d, reach, f) for f in range(5)])
 
 
 def one_hot(row, count):
@@ -135,6 +143,7 @@
     span_recv,
     hop_send,
     hop_recv,
+    far_sem,
 ):
     t = lax.axis_index("blk")
     slab = lax.axis_index("span")
@@ -154,12 +163,16 @@
             peers.append((pos, step, to))
 
     barrier = pltpu.get_barrier_semaphore()
-    for to in (after, before):
-        pl.semaphore_signal(barrier, inc=1, device_id={"blk": to}, device_id_type=MESH)
     for to in (above, below):
         pl.semaphore_signal(barrier, inc=1, device_id={"span": to}, device_id_type=MESH)
     for _, _, to in peers:
         pl.semaphore_signal(barrier, inc=1, device_id={"blk": to}, device_id_type=MESH)
+
+    is_first, is_last = digits[0] == 0, digits[0] == radices[0] - 1
+
+    @pl.when(is_first)
+    def _():
+        pl.semaphore_signal(barrier, inc=1, device_id={"blk": before}, device_id_type=MESH)
 
     def load(src):
         if src < 5:
@@ -179,7 +192,7 @@
     load_turn = pltpu.make_async_copy(turn_hbm, turn, load_sem.at[9, 2])
     load_offset = pltpu.make_async_copy(offset_hbm, offset, load_sem.at[9, 3])
     load_slot.start()
-    for src in (0, 1, 2, 3, 4, 5, 8, 6, 7):
+    for src in PACK_ORDER + (7, 6):
         for copy in load(src):
             copy.start()
     load_slopes.start()
@@ -192,13 +205,18 @@
     for end in range(2):
         pack[end, 0:1, :] = slot_row
 
-    for at, src in enumerate((0, 1, 2, 3, 4, 5, 8)):
+    for at, src in enumerate(PACK_ORDER):
         for copy in load(src):
             copy.wait()
         for end in range(2):
             pack[end, 1 + 25 * at : 26 + 25 * at, :] = cells(src, slice(100 * end, 100 * end + 25))
 
-    pl.semaphore_wait(barrier, 4 + len(peers))
+    pl.semaphore_wait(barrier, 2 + len(peers) + is_last.astype(I32))
+
+    @pl.when(is_last)
+    def _():
+        pl.semaphore_signal(far_sem, inc=1, device_id={"blk": after}, device_id_type=MESH)
+
 
     def circ(end, part):
         start, rows = CHUNKS[part]
@@ -211,8 +229,23 @@
             device_id_type=MESH,
         )
 
-    for end in range(2):
-        circ(end, 0).start()
+    def start_circ(*parts):
+        for part in parts:
+            circ(1, part).start()
+
+            @pl.when(jnp.logical_not(is_first))
+            def _():
+                circ(0, part).start()
+
+    def start_far(*parts):
+        @pl.when(is_first)
+        def _():
+            if parts[0] == 0:
+                pl.semaphore_wait(far_sem, 1)
+            for part in parts:
+                circ(0, part).start()
+
+    start_circ(0)
 
     for src in (6, 7):
         for copy in load(src):
@@ -255,8 +288,8 @@
     code = per_row([turn[0, s] for s in range(4)])
     shift = per_row([offset[s] for s in range(4)])
     shift = jnp.where(is_stator, shift, (nblk - shift) & (nblk - 1))
-    pair = [packet[:, :128], packet[:, 128:]]
-    pair = [jnp.where(is_stator, p, turned(p, code, True)) for p in pair]
+    own_pair = [packet[:, :128], packet[:, 128:]]
+    pair = [jnp.where(is_stator, p, turned(p, code, True)) for p in own_pair]
 
     def hop(number):
         pos, step, to = peers[number]
@@ -276,14 +309,38 @@
             if p == pos:
                 hop(number).start()
 
-    start_hops(0, pair)
-    for part in range(1, len(CHUNKS)):
-        for end in range(2):
-            circ(end, part).start()
+    def take_hops(pos, pair, distance):
+        for number, (p, step, _) in enumerate(peers):
+            if p == pos:
+                hop(number).wait()
+                for h in range(2):
+                    arrived = hops[number, :, 128 * h : 128 * h + 128]
+                    pair[h] = jnp.where(distance == step, arrived, pair[h])
+        return pair
+
+    r0, r1, r2 = radices
+    shift0 = lax.rem(shift, r0)
+    shift1 = lax.rem(shift // r0, r1)
+    move1 = lax.rem(shift1 + (digits[0] + shift0) // r0, r1)
+    carry0 = jnp.where(digits[0] < shift0, 1, 0)
+    source1 = lax.rem(digits[1] + 2 * r1 - shift1 - carry0, r1)
+    move2 = lax.rem(shift // (r0 * r1) + (source1 + shift1 + carry0) // r1, r2)
+
+    start_hops(1, pair)
+
+    @pl.when(jnp.logical_not(is_last))
+    def _():
+        circ(1, 1).start()
+
+    @pl.when(jnp.logical_not(is_first))
+    def _():
+        circ(0, 1).start()
+
 
     for kind in (1, 0):
         grid[kind] = moved(face[kind], table[...])
         sp_send[kind] = grid[kind, 0:224, 384 * kind : 384 * kind + 128]
+
 
     def span(end):
         return pltpu.make_async_remote_copy(
@@ -300,22 +357,6 @@
     for kind in (2, 3):
         grid[kind] = moved(face[kind], table[...])
 
-    carry = jnp.zeros((8, 128), I32)
-
-    def take_hops(pos, pair, carry):
-        radix = radices[pos]
-        digit = lax.rem(shift // weights[pos], radix) + carry
-        source = lax.rem(digits[pos] + 2 * radix - digit, radix)
-        next_carry = (source + digit - digits[pos]) // radix
-        distance = lax.rem(digit, radix)
-        for number, (p, step, _) in enumerate(peers):
-            if p == pos:
-                hop(number).wait()
-                for h in range(2):
-                    arrived = hops[number, :, 128 * h : 128 * h + 128]
-                    pair[h] = jnp.where(distance == step, arrived, pair[h])
-        return pair, next_carry
-
     load_slopes.wait()
     velocity = (5, 6, 7)
 
@@ -327,31 +368,29 @@
                 fx = fx + cells(8) * cells(1 + d)
             elif f == 1 + d:
                 fx = fx + cells(8) * cells(4)
-            part = jnp.dot(slopes[d], fx, precision=lax.Precision.HIGHEST, preferred_element_type=F32)
-            total = part if total is None else total + part
+            high, low = halves(fx)
+            for m, v in ((0, high), (0, low), (1, high)):
+                part = jnp.dot(slopes[m, d], v, preferred_element_type=F32)
+                total = part if total is None else total + part
         for b in range(4):
             acc[f, b] = total[:, 128 * b : 128 * b + 128]
 
-    todo = [[0, 1], [2, 3], [4]]
-    for pos in range(len(radices)):
-        for f in todo[pos] if pos < 3 else []:
-            volume(f)
-        pair, carry = take_hops(pos, pair, carry)
-        if pos + 1 < len(radices):
-            start_hops(pos + 1, pair)
-    for later in todo[len(radices) :]:
-        for f in later:
-            volume(f)
-
-    pair = [jnp.where(is_stator, turned(p, code, False), p) for p in pair]
-    arrived = jnp.concatenate(pair, axis=1)
-    put = jnp.where(lane == jnp.where(sub < 4, sub * 128 + HALF, (sub - 4) * 128 + HALF - 1), 1.0, 0.0)
-    first = jnp.where(sub < 4, put, 0.0), jnp.where(sub >= 4, put, 0.0)
-    tn = (((0,), (0,)), ((), ()))
-    spread = [
-        lax.dot_general(arrived, p, tn, precision=lax.Precision.HIGHEST, preferred_element_type=F32)
-        for p in first
-    ]
+    volume(0)
+    volume(1)
+    pair = take_hops(1, pair, move1)
+    start_hops(0, pair)
+
+    @pl.when(is_last)
+    def _():
+        circ(1, 1).start()
+
+    start_circ(2, 3)
+    start_far(0, 1)
+    for f in (2, 3, 4):
+        volume(f)
+    pair = take_hops(0, pair, shift0)
+    start_hops(2, pair)
+    start_far(2, 3)
 
     for end in range(2):
         span(end).wait()
@@ -390,53 +429,103 @@
             outer = []
             for f in range(7):
                 v = pltpu.roll(far[f], 127 if end else 1, axis=1)
-                v = jnp.where(
-                    axial == (HALF - 1 if end else HALF), spread[end][32 * f : 32 * f + 32, cols], v
-                )
                 edge = own[f] if f >= 5 else 0.0
                 outer.append(jnp.where(axial == (127 if end else 0), edge, v))
             diff, jump = face_parts(own if end else outer, outer if end else own, 2)
+            slides = axial == (HALF - 1 if end else HALF)
             for f in range(5):
                 value = diff[f] + jump[f] if end else diff[f] - jump[f]
-                corr[2 + end, 32 * f : 32 * f + 32, cols] = w * value
-
-    for kind in range(4):
-        back = moved(corr[kind], table[...], transposed=True)
-        grid[kind, 0:160, :] = back
-    for f in range(5):
-        for end in range(2):
+                corr[2 + end, 32 * f : 32 * f + 32, cols] = jnp.where(slides, 0.0, w * value)
+
+    def add_axial(end, values):
+        for f in range(5):
+            lines = pl.ds(4 * end, 25, stride=5)
+            for b in range(4):
+                part = values[32 * f : 32 * f + 25, 128 * b : 128 * b + 128]
+                acc[f, b, lines, :] = acc[f, b, lines, :] + part
+
+    for end in range(2):
+        back = moved(corr[end], table[...], transposed=True)
+        for f in range(5):
             for i in range(5):
                 rows = slice(25 * i + 20 * end, 25 * i + 20 * end + 5)
                 for b in range(4):
-                    cols = slice(128 * b, 128 * b + 128)
-                    acc[f, b, rows, :] += grid[end, 32 * f + 5 * i : 32 * f + 5 * i + 5, cols]
-            lines = pl.ds(4 * end, 25, stride=5)
-            for b in range(4):
-                cols = slice(128 * b, 128 * b + 128)
-                acc[f, b, lines, :] = acc[f, b, lines, :] + grid[2 + end, 32 * f : 32 * f + 25, cols]
-
-    w = 0.5 * metric_scale[0] / end_weight
-    for end in range(2):
-        for part in range(len(CHUNKS)):
-            circ(1 - end, part).wait_recv()
-            if part == 0:
-                other = one_hot(recv[end, 0:1, :], NB)
-                swap = lax.dot_general(other, table[...], dims, preferred_element_type=F32).astype(BF16)
-        near[end] = moved(recv[end], swap)
+                    part = back[32 * f + 5 * i : 32 * f + 5 * i + 5, 128 * b : 128 * b + 128]
+                    acc[f, b, rows, :] += part
+    for end in range(2):
+        add_axial(end, moved(corr[2 + end], table[...], transposed=True))
+
+    swaps = []
+    for end in range(2):
+        circ(1 - end, 0).wait_recv()
+        other = one_hot(recv[end, 0:1, :], NB)
+        swap = lax.dot_general(other, table[...], dims, preferred_element_type=F32)
+        swaps.append(swap.astype(BF16))
+    weight0 = 0.5 * metric_scale[0] / end_weight
+    sides = [None, None]
+
+    def settle(fields):
+        for end in range(2):
+            left, right, reach = sides[end]
+            rows = slice(100 * end, 100 * end + 25)
+            for f in fields:
+                diff, jump = face_value(left, right, 0, reach, f)
+                value = weight0 * (diff + jump if end else diff - jump)
+                for b in range(4):
+                    acc[f, b, rows, :] += value[:, 128 * b : 128 * b + 128]
+
+    def far_value(end, src):
+        at = PACK_ORDER.index(src)
+        return near[end, 1 + 25 * at : 26 + 25 * at, :]
+
+    def settle_rows(parts):
+        start, stop = CHUNKS[parts[0]][0], sum(CHUNKS[parts[-1]])
+        for end in range(2):
+            for part in parts:
+                if part > 0:
+                    circ(1 - end, part).wait_recv()
+            near[end, start:stop, :] = moved(recv[end, start:stop, :], swaps[end])
+
+    settle_rows((0, 1, 2))
+    for end in range(2):
         rows = slice(100 * end, 100 * end + 25)
-        own = [cells(src, rows) for src in (0, 1, 2, 3, 4, 5, 8)]
-        outer = [near[end, 1 + 25 * f : 26 + 25 * f, :] for f in range(7)]
-        diff, jump = face_parts(own if end else outer, outer if end else own, 0)
-        for f in range(5):
-            value = diff[f] + jump[f] if end else diff[f] - jump[f]
-            for b in range(4):
-                acc[f, b, rows, :] += w * value[:, 128 * b : 128 * b + 128]
-    for end in range(2):
-        for part in range(len(CHUNKS)):
-            circ(end, part).wait_send()
+        order = (0, 1, 2, 3, 4, 5, 8)
+        own = [cells(src, rows) for src in order]
+        other = [None if src == 3 else far_value(end, src) for src in order]
+        left, right = (own, other) if end else (other, own)
+        sides[end] = left, right, reach_of(left, right)
+    settle((0, 1, 2, 4))
+    pair = take_hops(2, pair, move2)
+    pair = [jnp.where(is_stator, turned(p, code, False), p) for p in pair]
+    outer = [pltpu.roll(p, 4, axis=0) for p in pair]
+    left = [jnp.where(is_stator, a, b) for a, b in zip(own_pair, outer)]
+    right = [jnp.where(is_stator, b, a) for a, b in zip(own_pair, outer)]
+
+    def values(pair):
+        return [pair[f // 4][:, 32 * (f % 4) : 32 * (f % 4) + 32] for f in range(7)]
+
+    diff, jump = face_parts(values(left), values(right), 2)
+    sign = jnp.where(is_stator[:, :32], w, -w)
+    fixes = jnp.concatenate([w * d + sign * j for d, j in zip(diff, jump)], axis=1)
+    fixes = jnp.concatenate(halves(fixes), axis=0)
+    tn = (((0,), (0,)), ((), ()))
+    for end in range(2):
+        mine = jnp.where(sub < 4 if end else sub >= 4, hot, 0.0).astype(BF16)
+        spread = lax.dot_general(
+            fixes, jnp.concatenate([mine, mine], axis=0), tn, preferred_element_type=F32
+        )
+        add_axial(end, spread)
+
+    settle_rows((3,))
+    for end in range(2):
+        sides[end][1 if end else 0][3] = far_value(end, 3)
+    settle((3,))
     for f in range(5):
         for b in range(4):
             rates[f, :, 128 * b : 128 * b + 128] = acc[f, b]
+    for end in range(2):
+        for part in range(len(CHUNKS)):
+            circ(end, part).wait_send()
 
 
 def on_device(mesh, radices, fields, section_store, mean_velocity, sound_speed, element_slot, face_turn, rotor_offset):
@@ -455,7 +544,7 @@
             pltpu.VMEM((9, 4, 125, 128), F32),
             pltpu.VMEM((5, 4, 125, 128), F32),
             pltpu.VMEM((1, NB), I32),
-            pltpu.VMEM((3, 125, 125), F32),
+            pltpu.VMEM((2, 3, 125, 125), BF16),
             pltpu.VMEM((NB, NB), BF16),
             pltpu.VMEM((2, PACK_ROWS, NB), F32),
             pltpu.VMEM((2, PACK_ROWS, NB), F32),
@@ -474,6 +563,7 @@
             dma((2,)),
             dma((hop_count,)),
             dma((hop_count,)),
+            pltpu.SemaphoreType.REGULAR,
         ],
         compiler_params=pltpu.CompilerParams(
             collective_id=0, has_side_effects=True, vmem_limit_bytes=40 * 2**20

time: 32.6 us -> 27.1 us (0.83)
  Pallas kernels: 29.8 us -> 24.4 us
    pallas_call x1, Pallas kernels: 29.8 us -> 24.4 us  [on_device(): pl.pallas_call(functools.partial(kernel, radices, nblk, nspan), out_shape...]
where the time goes in v2:
time: 27.1 us; the launch traced here: 27 us
  Pallas kernels  24.4 us (90%)
  other arithmetic  1.97 us (7%)
  between operations  0.67 us (2%)
    pallas_call x1, Pallas kernels, on_device(): pl.pallas_call(functools.partial(kernel, radices, nblk, nspan), out_shape...  24.4 us
    add x1, other arithmetic, on_device(): fields_next = fields + section_gain * store_next  1.97 us

profile of v2, /device:TPU:0, one launch (start us, length us, event | category | flops | bytes accessed | tf_op | source)
XLA Modules:
  0.0 27.0 jit_solution(17573459969392064167)
XLA Ops:
  0.6 0.0 copy-start
  0.6 0.0 copy-start.1
  0.7 24.4 %rates.1 = f32[5,125,512]{2,1,0:T(8,128)S(1)} custom-call(f32[5,125,512]{2,1,0:T(8,128)} %fields.1, f32[3,125,512]{2,1,0:T(8,128)} %mean.1, f32[125,512]{1,0:T(8,128)} %sound.1, s32[1,512]{1,0:T(1,128)} %bitcast.1, bf16[2,3,125,125]{3,2,1,0:T(8,128)(2,1)} %constant.8.clone.slopes_hbm, s32[1,4]{1,0:T(1,128)} %turn_hbm.1, s32[4]{0:T(128)} %offset_hbm.1), custom_call_target="tpu_custom_call" | custom-call | tf_op jit(solution)/shard_map/rates/pallas_call | solution.py:536
  25.0 0.0 copy-done
  25.0 0.0 copy-done.1
  25.0 2.0 %multiply_add_fusion = (f32[5,125,512]{2,1,0:T(8,128)}, f32[5,125,512]{2,1,0:T(8,128)}) fusion(f32[5,125,512]{2,1,0:T(8,128)S(1)} %copy-done, f32[5,125,512]{2,1,0:T(8,128)S(1)} %rates.1, f32[5,125,512]{2,1,0:T(8,128)S(1)} %copy-done.1), kind=kLoop, calls=%fused_computation | loop fusion | flops 1600000 | bytes 6400000 | tf_op jit(solution)/shard_map/add | solution.py:587
Async XLA Ops:
  0.6 24.4 %copy-start = (f32[5,125,512]{2,1,0:T(8,128)S(1)}, f32[5,125,512]{2,1,0:T(8,128)}, u32[]{:S(2)}) copy-start(f32[5,125,512]{2,1,0:T(8,128)} %fields.1) | copy-start | bytes 3840004
  0.6 24.4 %copy-start.1 = (f32[5,125,512]{2,1,0:T(8,128)S(1)}, f32[5,125,512]{2,1,0:T(8,128)}, u32[]{:S(2)}) copy-start(f32[5,125,512]{2,1,0:T(8,128)} %param.9) | copy-start | bytes 3840004

commit v3 on v2

--- a/solution.py
+++ b/solution.py
@@ -134,8 +134,12 @@
     corr,
     sp_send,
     sp_recv,
-    stage,
+    own_packet,
+    gathered,
+    bundle,
     hops,
+    final_out,
+    final_in,
     load_sem,
     circ_send,
     circ_recv,
@@ -143,6 +147,8 @@
     span_recv,
     hop_send,
     hop_recv,
+    plane_send,
+    plane_recv,
     far_sem,
 ):
     t = lax.axis_index("blk")
@@ -150,25 +156,32 @@
     after, before = lax.rem(t + 1, nblk), lax.rem(t + nblk - 1, nblk)
     above, below = lax.rem(slab + 1, nspan), lax.rem(slab + nspan - 1, nspan)
 
-    digits, weights, rest, weight = [], [], t, 1
-    for radix in radices:
-        digits.append(lax.rem(rest, radix))
-        weights.append(weight)
-        rest = rest // radix
-        weight *= radix
-    peers = []
-    for pos, radix in enumerate(radices):
-        for step in range(1, radix):
-            to = t + (lax.rem(digits[pos] + step, radix) - digits[pos]) * weights[pos]
-            peers.append((pos, step, to))
+    r0, r1, r2 = radices
+    z, y, x_at = lax.rem(t, r0), lax.rem(t // r0, r1), t // (r0 * r1)
+    is_first, is_last = z == 0, z == r0 - 1
+    inner = jnp.logical_and(z > 0, z < r0 - 1)
+    run = [t + (lax.rem(z + step, r0) - z) for step in range(1, r0)]
+    across = [jnp.logical_and(z == 0, step == r0 - 1) | jnp.logical_and(z == r0 - 1, step == 1) for step in range(1, r0)]
+    plane = []
+    for dy in range(r1):
+        for dx in range(r2):
+            if dy or dx:
+                to = z + r0 * lax.rem(y + dy, r1) + r0 * r1 * lax.rem(x_at + dx, r2)
+                plane.append((dy, dx, to))
 
     barrier = pltpu.get_barrier_semaphore()
     for to in (above, below):
         pl.semaphore_signal(barrier, inc=1, device_id={"span": to}, device_id_type=MESH)
-    for _, _, to in peers:
-        pl.semaphore_signal(barrier, inc=1, device_id={"blk": to}, device_id_type=MESH)
-
-    is_first, is_last = digits[0] == 0, digits[0] == radices[0] - 1
+    for to, skip in zip(run, across):
+
+        @pl.when(jnp.logical_not(skip))
+        def _():
+            pl.semaphore_signal(barrier, inc=1, device_id={"blk": to}, device_id_type=MESH)
+
+    @pl.when(inner)
+    def _():
+        for _, _, to in plane:
+            pl.semaphore_signal(barrier, inc=1, device_id={"blk": to}, device_id_type=MESH)
 
     @pl.when(is_first)
     def _():
@@ -205,13 +218,19 @@
     for end in range(2):
         pack[end, 0:1, :] = slot_row
 
+    lane = lax.broadcasted_iota(I32, (8, NB), 1)
+    sub = lax.broadcasted_iota(I32, (8, NB), 0)
+    wanted = jnp.where(sub < 4, sub * 128 + (HALF - 1), (sub - 4) * 128 + HALF)
+    column = jnp.sum(jnp.where(lane == wanted, slot_row, 0.0), axis=1, keepdims=True)
+    hot = jnp.where(lane.astype(F32) == column, 1.0, 0.0)
+
     for at, src in enumerate(PACK_ORDER):
         for copy in load(src):
             copy.wait()
         for end in range(2):
             pack[end, 1 + 25 * at : 26 + 25 * at, :] = cells(src, slice(100 * end, 100 * end + 25))
 
-    pl.semaphore_wait(barrier, 2 + len(peers) + is_last.astype(I32))
+    pl.semaphore_wait(barrier, jnp.where(inner, 2 + r0 - 1 + len(plane), r0 + is_last.astype(I32)))
 
     @pl.when(is_last)
     def _():
@@ -231,19 +250,21 @@
 
     def start_circ(*parts):
         for part in parts:
-            circ(1, part).start()
+
+            @pl.when(jnp.logical_not(is_last))
+            def _():
+                circ(1, part).start()
 
             @pl.when(jnp.logical_not(is_first))
             def _():
                 circ(0, part).start()
 
-    def start_far(*parts):
-        @pl.when(is_first)
-        def _():
-            if parts[0] == 0:
-                pl.semaphore_wait(far_sem, 1)
-            for part in parts:
-                circ(0, part).start()
+    every = range(len(CHUNKS))
+
+    @pl.when(is_last)
+    def _():
+        for part in every:
+            circ(1, part).start()
 
     start_circ(0)
 
@@ -261,11 +282,6 @@
                         rows = slice(25 * i + 20 * end, 25 * i + 20 * end + 5)
                         face[kind, 32 * at + 5 * i : 32 * at + 5 * i + 5, :] = cells(src, rows)
 
-    lane = lax.broadcasted_iota(I32, (8, NB), 1)
-    sub = lax.broadcasted_iota(I32, (8, NB), 0)
-    wanted = jnp.where(sub < 4, sub * 128 + (HALF - 1), (sub - 4) * 128 + HALF)
-    column = jnp.sum(jnp.where(lane == wanted, slot_row, 0.0), axis=1, keepdims=True)
-    hot = jnp.where(lane.astype(F32) == column, 1.0, 0.0)
     dims = (((1,), (1,)), ((), ()))
     packet = jnp.zeros((8, 256), F32)
     for kind, rows in ((3, sub < 4), (2, sub >= 4)):
@@ -291,51 +307,100 @@
     own_pair = [packet[:, :128], packet[:, 128:]]
     pair = [jnp.where(is_stator, p, turned(p, code, True)) for p in own_pair]
 
-    def hop(number):
-        pos, step, to = peers[number]
+    for h in range(2):
+        own_packet[:, 128 * h : 128 * h + 128] = pair[h]
+
+    def collect(to_z, from_z):
         return pltpu.make_async_remote_copy(
-            src_ref=stage.at[pos],
-            dst_ref=hops.at[number],
-            send_sem=hop_send.at[number],
-            recv_sem=hop_recv.at[number],
-            device_id={"blk": to},
+            src_ref=own_packet,
+            dst_ref=gathered.at[from_z],
+            send_sem=hop_send.at[to_z],
+            recv_sem=hop_recv.at[from_z],
+            device_id={"blk": t + to_z - z},
             device_id_type=MESH,
         )
 
-    def start_hops(pos, pair):
+    for to_z in range(1, r0 - 1):
+
+        @pl.when(z != to_z)
+        def _():
+            collect(to_z, z).start()
+
+    start_circ(1, 2, 3)
+
+    def take_collected():
+        @pl.when(inner)
+        def _():
+            for from_z in range(r0):
+
+                @pl.when(z != from_z)
+                def _():
+                    collect(1, from_z).wait_recv()
+
+        for to_z in range(1, r0 - 1):
+
+            @pl.when(z != to_z)
+            def _():
+                collect(to_z, 0).wait_send()
+
         for h in range(2):
-            stage[pos, :, 128 * h : 128 * h + 128] = pair[h]
-        for number, (p, _, _) in enumerate(peers):
-            if p == pos:
-                hop(number).start()
-
-    def take_hops(pos, pair, distance):
-        for number, (p, step, _) in enumerate(peers):
-            if p == pos:
-                hop(number).wait()
-                for h in range(2):
-                    arrived = hops[number, :, 128 * h : 128 * h + 128]
-                    pair[h] = jnp.where(distance == step, arrived, pair[h])
-        return pair
-
-    r0, r1, r2 = radices
+            lanes = slice(128 * h, 128 * h + 128)
+            for half, target in enumerate((z, outer_z)):
+                source = lax.rem(target + r0 - shift0, r0)
+                value = pair[h]
+                for from_z in range(r0):
+                    value = jnp.where((source == from_z) & (z != from_z), gathered[from_z, :, lanes], value)
+                bundle[8 * half : 8 * half + 8, lanes] = value
+
+    outer_z = jnp.where(z == 1, 0, r0 - 1)
     shift0 = lax.rem(shift, r0)
     shift1 = lax.rem(shift // r0, r1)
-    move1 = lax.rem(shift1 + (digits[0] + shift0) // r0, r1)
-    carry0 = jnp.where(digits[0] < shift0, 1, 0)
-    source1 = lax.rem(digits[1] + 2 * r1 - shift1 - carry0, r1)
-    move2 = lax.rem(shift // (r0 * r1) + (source1 + shift1 + carry0) // r1, r2)
-
-    start_hops(1, pair)
-
-    @pl.when(jnp.logical_not(is_last))
-    def _():
-        circ(1, 1).start()
-
-    @pl.when(jnp.logical_not(is_first))
-    def _():
-        circ(0, 1).start()
-
+    shift2 = shift // (r0 * r1)
+
+    def hop(number):
+        return pltpu.make_async_remote_copy(
+            src_ref=bundle,
+            dst_ref=hops.at[number],
+            send_sem=plane_send.at[number],
+            recv_sem=plane_recv.at[number],
+            device_id={"blk": plane[number][2]},
+            device_id_type=MESH,
+        )
+
+    def start_plane():
+        @pl.when(inner)
+        def _():
+            for number in range(len(plane)):
+                hop(number).start()
+
+    def take_plane():
+        @pl.when(inner)
+        def _():
+            for number in range(len(plane)):
+                hop(number).wait()
+
+        for half, target in enumerate((z, outer_z)):
+            up1 = shift1 + jnp.where(target < shift0, 1, 0)
+            source1 = lax.rem(y + 2 * r1 - up1, r1)
+            move1 = lax.rem(up1, r1)
+            move2 = lax.rem(shift2 + (source1 + up1) // r1, r2)
+            for h in range(2):
+                lanes = slice(128 * h, 128 * h + 128)
+                rows = slice(8 * half, 8 * half + 8)
+                value = bundle[rows, lanes]
+                for number, (dy, dx, _) in enumerate(plane):
+                    value = jnp.where((move1 == dy) & (move2 == dx), hops[number, rows, lanes], value)
+                final_out[half, :, lanes] = value
+
+    def deliver():
+        return pltpu.make_async_remote_copy(
+            src_ref=final_out.at[1],
+            dst_ref=final_in,
+            send_sem=hop_send.at[0],
+            recv_sem=hop_send.at[r0 - 1],
+            device_id={"blk": lax.rem(t + jnp.where(z == 1, nblk - 1, 1), nblk)},
+            device_id_type=MESH,
+        )
 
     for kind in (1, 0):
         grid[kind] = moved(face[kind], table[...])
@@ -377,20 +442,17 @@
 
     volume(0)
     volume(1)
-    pair = take_hops(1, pair, move1)
-    start_hops(0, pair)
-
-    @pl.when(is_last)
-    def _():
-        circ(1, 1).start()
-
-    start_circ(2, 3)
-    start_far(0, 1)
+    take_collected()
+    start_plane()
+
+    @pl.when(is_first)
+    def _():
+        pl.semaphore_wait(far_sem, 1)
+        for part in every:
+            circ(0, part).start()
+
     for f in (2, 3, 4):
         volume(f)
-    pair = take_hops(0, pair, shift0)
-    start_hops(2, pair)
-    start_far(2, 3)
 
     for end in range(2):
         span(end).wait()
@@ -486,6 +548,12 @@
                     circ(1 - end, part).wait_recv()
             near[end, start:stop, :] = moved(recv[end, start:stop, :], swaps[end])
 
+    take_plane()
+
+    @pl.when(inner)
+    def _():
+        deliver().start()
+
     settle_rows((0, 1, 2))
     for end in range(2):
         rows = slice(100 * end, 100 * end + 25)
@@ -495,7 +563,18 @@
         left, right = (own, other) if end else (other, own)
         sides[end] = left, right, reach_of(left, right)
     settle((0, 1, 2, 4))
-    pair = take_hops(2, pair, move2)
+    settle_rows((3,))
+    for end in range(2):
+        sides[end][1 if end else 0][3] = far_value(end, 3)
+    settle((3,))
+    @pl.when(jnp.logical_not(inner))
+    def _():
+        deliver().wait_recv()
+
+    pair = []
+    for h in range(2):
+        lanes = slice(128 * h, 128 * h + 128)
+        pair.append(jnp.where(inner, final_out[0, :, lanes], final_in[:, lanes]))
     pair = [jnp.where(is_stator, turned(p, code, False), p) for p in pair]
     outer = [pltpu.roll(p, 4, axis=0) for p in pair]
     left = [jnp.where(is_stator, a, b) for a, b in zip(own_pair, outer)]
@@ -516,10 +595,6 @@
         )
         add_axial(end, spread)
 
-    settle_rows((3,))
-    for end in range(2):
-        sides[end][1 if end else 0][3] = far_value(end, 3)
-    settle((3,))
     for f in range(5):
         for b in range(4):
             rates[f, :, 128 * b : 128 * b + 128] = acc[f, b]
@@ -527,10 +602,14 @@
         for part in range(len(CHUNKS)):
             circ(end, part).wait_send()
 
+    @pl.when(inner)
+    def _():
+        deliver().wait_send()
+
 
 def on_device(mesh, radices, fields, section_store, mean_velocity, sound_speed, element_slot, face_turn, rotor_offset):
     nblk, nspan = mesh.shape["blk"], mesh.shape["span"]
-    hop_count = sum(r - 1 for r in radices)
+    r0, r1, r2 = radices
     anywhere = pl.BlockSpec(memory_space=pltpu.HBM)
     dma = pltpu.SemaphoreType.DMA
     rates = pl.pallas_call(
@@ -554,15 +633,21 @@
             pltpu.VMEM((4, 160, NB), F32),
             pltpu.VMEM((2, 224, 128), F32),
             pltpu.VMEM((2, 224, 128), F32),
-            pltpu.VMEM((len(radices), 8, 256), F32),
-            pltpu.VMEM((hop_count, 8, 256), F32),
+            pltpu.VMEM((8, 256), F32),
+            pltpu.VMEM((r0, 8, 256), F32),
+            pltpu.VMEM((16, 256), F32),
+            pltpu.VMEM((r1 * r2 - 1, 16, 256), F32),
+            pltpu.VMEM((2, 8, 256), F32),
+            pltpu.VMEM((8, 256), F32),
             dma((10, 4)),
             dma((2, len(CHUNKS))),
             dma((2, len(CHUNKS))),
             dma((2,)),
             dma((2,)),
-            dma((hop_count,)),
-            dma((hop_count,)),
+            dma((r0,)),
+            dma((r0,)),
+            dma((r1 * r2 - 1,)),
+            dma((r1 * r2 - 1,)),
             pltpu.SemaphoreType.REGULAR,
         ],
         compiler_params=pltpu.CompilerParams(

time: 27.1 us -> 24.7 us (0.911)
  Pallas kernels: 24.4 us -> 21.9 us
    pallas_call x1, Pallas kernels: 24.4 us -> 21.9 us  [on_device(): pl.pallas_call(functools.partial(kernel, radices, nblk, nspan), out_shape...]
where the time goes in v3:
time: 24.7 us; the launch traced here: 24.6 us
  Pallas kernels  21.9 us (89%)
  other arithmetic  1.97 us (8%)
  between operations  0.67 us (3%)
    pallas_call x1, Pallas kernels, on_device(): pl.pallas_call(functools.partial(kernel, radices, nblk, nspan), out_shape...  21.9 us
    add x1, other arithmetic, on_device(): fields_next = fields + section_gain * store_next  1.97 us

profile of v3, /device:TPU:0, one launch (start us, length us, event | category | flops | bytes accessed | tf_op | source)
XLA Modules:
  0.0 24.6 jit_solution(6508866425998072440)
XLA Ops:
  0.6 0.0 copy-start
  0.6 0.0 copy-start.1
  0.7 21.9 %rates.1 = f32[5,125,512]{2,1,0:T(8,128)S(1)} custom-call(f32[5,125,512]{2,1,0:T(8,128)} %fields.1, f32[3,125,512]{2,1,0:T(8,128)} %mean.1, f32[125,512]{1,0:T(8,128)} %sound.1, s32[1,512]{1,0:T(1,128)} %bitcast.1, bf16[2,3,125,125]{3,2,1,0:T(8,128)(2,1)} %constant.8.clone.slopes_hbm, s32[1,4]{1,0:T(1,128)} %turn_hbm.1, s32[4]{0:T(128)} %offset_hbm.1), custom_call_target="tpu_custom_call" | custom-call | tf_op jit(solution)/shard_map/rates/pallas_call | solution.py:615
  22.6 0.0 copy-done
  22.6 0.0 copy-done.1
  22.6 2.0 %multiply_add_fusion = (f32[5,125,512]{2,1,0:T(8,128)}, f32[5,125,512]{2,1,0:T(8,128)}) fusion(f32[5,125,512]{2,1,0:T(8,128)S(1)} %copy-done, f32[5,125,512]{2,1,0:T(8,128)S(1)} %rates.1, f32[5,125,512]{2,1,0:T(8,128)S(1)} %copy-done.1), kind=kLoop, calls=%fused_computation | loop fusion | flops 1600000 | bytes 6400000 | tf_op jit(solution)/shard_map/add | solution.py:672
Async XLA Ops:
  0.6 22.0 %copy-start = (f32[5,125,512]{2,1,0:T(8,128)S(1)}, f32[5,125,512]{2,1,0:T(8,128)}, u32[]{:S(2)}) copy-start(f32[5,125,512]{2,1,0:T(8,128)} %fields.1) | copy-start | bytes 3840004
  0.6 22.0 %copy-start.1 = (f32[5,125,512]{2,1,0:T(8,128)S(1)}, f32[5,125,512]{2,1,0:T(8,128)}, u32[]{:S(2)}) copy-start(f32[5,125,512]{2,1,0:T(8,128)} %param.9) | copy-start | bytes 3840004

commit v4 on v3

--- a/solution.py
+++ b/solution.py
@@ -44,7 +44,7 @@
 def slope_matrices():
     d, e = lobatto_slopes(), np.eye(5)
     full = [np.kron(np.kron(d, e), e), np.kron(np.kron(e, d), e), np.kron(np.kron(e, e), d)]
-    full = np.stack([-g * m for g, m in zip(metric_scale, full)])
+    full = np.stack([-time_step * g * m for g, m in zip(metric_scale, full)])
     high = full.astype(BF16)
     return np.stack([high, (full - high.astype(np.float64)).astype(BF16)])
 
@@ -112,23 +112,26 @@
     nblk,
     nspan,
     fields,
+    store,
     mean,
     sound,
     slot_hbm,
     slopes_hbm,
     turn_hbm,
     offset_hbm,
-    rates,
+    acc,
+    fixed,
     turn,
     offset,
     x,
-    acc,
+    old,
     slot,
     slopes,
     table,
     pack,
     recv,
     near,
+    swaps,
     face,
     grid,
     corr,
@@ -141,6 +144,7 @@
     final_out,
     final_in,
     load_sem,
+    old_sem,
     circ_send,
     circ_recv,
     span_send,
@@ -193,30 +197,75 @@
         else:
             array = mean.at[src - 5] if src < 8 else sound
         return [
-            pltpu.make_async_copy(array.at[:, pl.ds(128 * b, 128)], x.at[src, b], load_sem.at[src, b])
+            pltpu.make_async_copy(array.at[:, pl.ds(128 * b, 128)], x.at[src, b], load_sem.at[src])
             for b in range(4)
         ]
 
+    def arrived_all(ref, sem):
+        pltpu.make_async_copy(ref, ref, sem).wait()
+
+    def loaded(src):
+        arrived_all(x.at[src], load_sem.at[src])
+
     def cells(src, rows=slice(0, 125)):
         return jnp.concatenate([x[src, b, rows, :] for b in range(4)], axis=1)
 
-    load_slot = pltpu.make_async_copy(slot_hbm, slot, load_sem.at[9, 0])
-    load_slopes = pltpu.make_async_copy(slopes_hbm, slopes, load_sem.at[9, 1])
-    load_turn = pltpu.make_async_copy(turn_hbm, turn, load_sem.at[9, 2])
-    load_offset = pltpu.make_async_copy(offset_hbm, offset, load_sem.at[9, 3])
+    load_slot = pltpu.make_async_copy(slot_hbm, slot, load_sem.at[9])
+    load_slopes = pltpu.make_async_copy(slopes_hbm, slopes, load_sem.at[10])
+    load_turn = pltpu.make_async_copy(turn_hbm, turn, load_sem.at[11])
+    load_offset = pltpu.make_async_copy(offset_hbm, offset, load_sem.at[12])
     load_slot.start()
     for src in PACK_ORDER + (7, 6):
         for copy in load(src):
             copy.start()
     load_slopes.start()
+    for f in range(5):
+        for b in range(4):
+            pltpu.make_async_copy(
+                store.at[f, :, pl.ds(128 * b, 128)], old.at[f, b], old_sem.at[f]
+            ).start()
     load_turn.start()
     load_offset.start()
 
     load_slot.wait()
     slot_row = slot[...].astype(F32)
-    table[...] = one_hot(slot_row, NB)
     for end in range(2):
         pack[end, 0:1, :] = slot_row
+
+    def circ(end, part):
+        start, rows = CHUNKS[part]
+        return pltpu.make_async_remote_copy(
+            src_ref=pack.at[end, pl.ds(start, rows), :],
+            dst_ref=recv.at[1 - end, pl.ds(start, rows), :],
+            send_sem=circ_send.at[end],
+            recv_sem=circ_recv.at[1 - end, part],
+            device_id={"blk": after if end == 1 else before},
+            device_id_type=MESH,
+        )
+
+    def start_circ(*parts):
+        for part in parts:
+
+            @pl.when(jnp.logical_not(is_last))
+            def _():
+                circ(1, part).start()
+
+            @pl.when(jnp.logical_not(is_first))
+            def _():
+                circ(0, part).start()
+
+    every = range(len(CHUNKS))
+
+    for at, src in enumerate(PACK_ORDER):
+        loaded(src)
+        pack[1, 1 + 25 * at : 26 + 25 * at, :] = cells(src, slice(100, 125))
+
+    @pl.when(is_last)
+    def _():
+        pl.semaphore_wait(barrier, r0 + 1)
+        pl.semaphore_signal(far_sem, inc=1, device_id={"blk": after}, device_id_type=MESH)
+        for part in every:
+            circ(1, part).start()
 
     lane = lax.broadcasted_iota(I32, (8, NB), 1)
     sub = lax.broadcasted_iota(I32, (8, NB), 0)
@@ -224,54 +273,8 @@
     column = jnp.sum(jnp.where(lane == wanted, slot_row, 0.0), axis=1, keepdims=True)
     hot = jnp.where(lane.astype(F32) == column, 1.0, 0.0)
 
-    for at, src in enumerate(PACK_ORDER):
-        for copy in load(src):
-            copy.wait()
-        for end in range(2):
-            pack[end, 1 + 25 * at : 26 + 25 * at, :] = cells(src, slice(100 * end, 100 * end + 25))
-
-    pl.semaphore_wait(barrier, jnp.where(inner, 2 + r0 - 1 + len(plane), r0 + is_last.astype(I32)))
-
-    @pl.when(is_last)
-    def _():
-        pl.semaphore_signal(far_sem, inc=1, device_id={"blk": after}, device_id_type=MESH)
-
-
-    def circ(end, part):
-        start, rows = CHUNKS[part]
-        return pltpu.make_async_remote_copy(
-            src_ref=pack.at[end, pl.ds(start, rows), :],
-            dst_ref=recv.at[1 - end, pl.ds(start, rows), :],
-            send_sem=circ_send.at[end, part],
-            recv_sem=circ_recv.at[1 - end, part],
-            device_id={"blk": after if end == 1 else before},
-            device_id_type=MESH,
-        )
-
-    def start_circ(*parts):
-        for part in parts:
-
-            @pl.when(jnp.logical_not(is_last))
-            def _():
-                circ(1, part).start()
-
-            @pl.when(jnp.logical_not(is_first))
-            def _():
-                circ(0, part).start()
-
-    every = range(len(CHUNKS))
-
-    @pl.when(is_last)
-    def _():
-        for part in every:
-            circ(1, part).start()
-
-    start_circ(0)
-
-    for src in (6, 7):
-        for copy in load(src):
-            copy.wait()
-    for d in (2, 1):
+    loaded(7)
+    def pack_faces(d):
         for at, src in enumerate((0, 1, 2, 3, 4, 4 + 1 + d, 8)):
             for end in range(2):
                 kind = 2 * (d - 1) + end
@@ -282,6 +285,7 @@
                         rows = slice(25 * i + 20 * end, 25 * i + 20 * end + 5)
                         face[kind, 32 * at + 5 * i : 32 * at + 5 * i + 5, :] = cells(src, rows)
 
+    pack_faces(2)
     dims = (((1,), (1,)), ((), ()))
     packet = jnp.zeros((8, 256), F32)
     for kind, rows in ((3, sub < 4), (2, sub >= 4)):
@@ -320,13 +324,23 @@
             device_id_type=MESH,
         )
 
+    @pl.when(jnp.logical_not(is_last))
+    def _():
+        pl.semaphore_wait(barrier, jnp.where(inner, 2 + r0 - 1 + len(plane), r0))
+
     for to_z in range(1, r0 - 1):
 
         @pl.when(z != to_z)
         def _():
             collect(to_z, z).start()
 
-    start_circ(1, 2, 3)
+    for at, src in enumerate(PACK_ORDER):
+        pack[0, 1 + 25 * at : 26 + 25 * at, :] = cells(src, slice(0, 25))
+    start_circ(*every)
+
+    table[...] = one_hot(slot_row, NB)
+    loaded(6)
+    pack_faces(1)
 
     def take_collected():
         @pl.when(inner)
@@ -361,8 +375,8 @@
         return pltpu.make_async_remote_copy(
             src_ref=bundle,
             dst_ref=hops.at[number],
-            send_sem=plane_send.at[number],
-            recv_sem=plane_recv.at[number],
+            send_sem=plane_send.at[0],
+            recv_sem=plane_recv.at[0],
             device_id={"blk": plane[number][2]},
             device_id_type=MESH,
         )
@@ -376,8 +390,8 @@
     def take_plane():
         @pl.when(inner)
         def _():
-            for number in range(len(plane)):
-                hop(number).wait()
+            arrived_all(hops, plane_send.at[0])
+            arrived_all(hops, plane_recv.at[0])
 
         for half, target in enumerate((z, outer_z)):
             up1 = shift1 + jnp.where(target < shift0, 1, 0)
@@ -404,28 +418,49 @@
 
     for kind in (1, 0):
         grid[kind] = moved(face[kind], table[...])
-        sp_send[kind] = grid[kind, 0:224, 384 * kind : 384 * kind + 128]
+        for f in range(7):
+            sp_send[kind, 25 * f : 25 * f + 25, :] = grid[
+                kind, 32 * f : 32 * f + 25, 384 * kind : 384 * kind + 128
+            ]
 
 
     def span(end):
         return pltpu.make_async_remote_copy(
             src_ref=sp_send.at[end],
-            dst_ref=sp_recv.at[1 - end],
+            dst_ref=sp_recv.at[1 - end, pl.ds(0, PACK_ROWS), :],
             send_sem=span_send.at[end],
             recv_sem=span_recv.at[1 - end],
             device_id={"span": above if end == 1 else below},
             device_id_type=MESH,
         )
 
-    for end in range(2):
-        span(end).start()
+    has_below, has_above = slab > 0, slab < nspan - 1
+
+    @pl.when(has_above)
+    def _():
+        span(1).start()
+
+    @pl.when(has_below)
+    def _():
+        span(0).start()
+
     for kind in (2, 3):
         grid[kind] = moved(face[kind], table[...])
 
+    def span_sent():
+        @pl.when(has_above)
+        def _():
+            span(1).wait_send()
+
+        @pl.when(has_below)
+        def _():
+            span(0).wait_send()
+
     load_slopes.wait()
     velocity = (5, 6, 7)
 
     def volume(f):
+        arrived_all(old.at[f], old_sem.at[f])
         total = None
         for d in range(3):
             fx = cells(velocity[d]) * cells(f)
@@ -438,49 +473,24 @@
                 part = jnp.dot(slopes[m, d], v, preferred_element_type=F32)
                 total = part if total is None else total + part
         for b in range(4):
-            acc[f, b] = total[:, 128 * b : 128 * b + 128]
+            acc[f, b] = section_decay * old[f, b] + total[:, 128 * b : 128 * b + 128]
 
     volume(0)
     volume(1)
-    take_collected()
-    start_plane()
-
     @pl.when(is_first)
     def _():
+        span_sent()
         pl.semaphore_wait(far_sem, 1)
         for part in every:
             circ(0, part).start()
 
+    take_collected()
+    start_plane()
+
     for f in (2, 3, 4):
         volume(f)
 
-    for end in range(2):
-        span(end).wait()
-    w = 0.5 * metric_scale[1] / end_weight
-    for b in range(5):
-        left, right = [], []
-        for f in range(7):
-            rows = slice(32 * f, 32 * f + 32)
-            if b > 0:
-                left.append(grid[1, rows, 128 * b - 128 : 128 * b])
-            if b < 4:
-                right.append(grid[0, rows, 128 * b : 128 * b + 128])
-        for f in range(7):
-            rows = slice(32 * f, 32 * f + 32)
-            if b == 0:
-                wall = -right[f] if f == 2 else right[f]
-                left.append(jnp.where(slab > 0, sp_recv[0, rows, :], wall))
-            if b == 4:
-                wall = -left[f] if f == 2 else left[f]
-                right.append(jnp.where(slab < nspan - 1, sp_recv[1, rows, :], wall))
-        diff, jump = face_parts(left, right, 1)
-        for f in range(5):
-            if b > 0:
-                corr[1, 32 * f : 32 * f + 32, 128 * b - 128 : 128 * b] = w * (diff[f] + jump[f])
-            if b < 4:
-                corr[0, 32 * f : 32 * f + 32, 128 * b : 128 * b + 128] = w * (diff[f] - jump[f])
-
-    w = 0.5 * metric_scale[2] / end_weight
+    w = 0.5 * time_step * metric_scale[2] / end_weight
     axial = lax.broadcasted_iota(I32, (32, 128), 1)
     for s in range(4):
         cols = slice(128 * s, 128 * s + 128)
@@ -507,6 +517,80 @@
                 acc[f, b, lines, :] = acc[f, b, lines, :] + part
 
     for end in range(2):
+        add_axial(end, moved(corr[2 + end], table[...], transposed=True))
+
+    far_end = jnp.where(is_last, 1, 0)
+    near_end = 1 - far_end
+    weight0 = 0.5 * time_step * metric_scale[0] / end_weight
+
+    def settle_rows(end, parts):
+        start, stop = CHUNKS[parts[0]][0], sum(CHUNKS[parts[-1]])
+        for part in parts:
+            first, rows = CHUNKS[part]
+            arrived_all(recv.at[end, pl.ds(first, rows), :], circ_recv.at[end, part])
+            if part == 0:
+                other = one_hot(recv[end, 0:1, :], NB)
+                swap = lax.dot_general(other, table[...], dims, preferred_element_type=F32)
+                swaps[end] = swap.astype(BF16)
+        near[end, start:stop, :] = moved(recv[end, start:stop, :], swaps[end])
+
+    def settle(end, fields, reach=None):
+        def side(ref, src):
+            at = PACK_ORDER.index(src)
+            return ref[end, 1 + 25 * at : 26 + 25 * at, :]
+
+        order = (0, 1, 2, 3, 4, 5, 8)
+        own = [side(pack, src) for src in order]
+        other = [side(near, src) if src != 3 or 3 in fields else None for src in order]
+        if reach is None:
+            reach = reach_of(own, other)
+        sign = jnp.where(end == 0, weight0, -weight0)
+        for f in fields:
+            diff, jump = face_value(other, own, 0, reach, f)
+            fixed[end, f, 0:25, :] = sign * diff - weight0 * jump
+        return reach
+
+    take_plane()
+
+    @pl.when(inner)
+    def _():
+        deliver().start()
+
+    settle_rows(near_end, (0, 1, 2, 3))
+    settle(near_end, (0, 1, 2, 3, 4))
+    @pl.when(has_above)
+    def _():
+        span(0).wait_recv()
+
+    @pl.when(has_below)
+    def _():
+        span(1).wait_recv()
+
+    w = 0.5 * time_step * metric_scale[1] / end_weight
+    for b in range(5):
+        left, right = [], []
+        for f in range(7):
+            rows = slice(32 * f, 32 * f + 32)
+            if b > 0:
+                left.append(grid[1, rows, 128 * b - 128 : 128 * b])
+            if b < 4:
+                right.append(grid[0, rows, 128 * b : 128 * b + 128])
+        for f in range(7):
+            rows = slice(32 * f, 32 * f + 32)
+            if b == 0:
+                wall = -right[f] if f == 2 else right[f]
+                left.append(jnp.where(has_below, sp_recv[0, 25 * f : 25 * f + 32, :], wall))
+            if b == 4:
+                wall = -left[f] if f == 2 else left[f]
+                right.append(jnp.where(has_above, sp_recv[1, 25 * f : 25 * f + 32, :], wall))
+        diff, jump = face_parts(left, right, 1)
+        for f in range(5):
+            if b > 0:
+                corr[1, 32 * f : 32 * f + 32, 128 * b - 128 : 128 * b] = w * (diff[f] + jump[f])
+            if b < 4:
+                corr[0, 32 * f : 32 * f + 32, 128 * b : 128 * b + 128] = w * (diff[f] - jump[f])
+
+    for end in range(2):
         back = moved(corr[end], table[...], transposed=True)
         for f in range(5):
             for i in range(5):
@@ -514,59 +598,11 @@
                 for b in range(4):
                     part = back[32 * f + 5 * i : 32 * f + 5 * i + 5, 128 * b : 128 * b + 128]
                     acc[f, b, rows, :] += part
-    for end in range(2):
-        add_axial(end, moved(corr[2 + end], table[...], transposed=True))
-
-    swaps = []
-    for end in range(2):
-        circ(1 - end, 0).wait_recv()
-        other = one_hot(recv[end, 0:1, :], NB)
-        swap = lax.dot_general(other, table[...], dims, preferred_element_type=F32)
-        swaps.append(swap.astype(BF16))
-    weight0 = 0.5 * metric_scale[0] / end_weight
-    sides = [None, None]
-
-    def settle(fields):
-        for end in range(2):
-            left, right, reach = sides[end]
-            rows = slice(100 * end, 100 * end + 25)
-            for f in fields:
-                diff, jump = face_value(left, right, 0, reach, f)
-                value = weight0 * (diff + jump if end else diff - jump)
-                for b in range(4):
-                    acc[f, b, rows, :] += value[:, 128 * b : 128 * b + 128]
-
-    def far_value(end, src):
-        at = PACK_ORDER.index(src)
-        return near[end, 1 + 25 * at : 26 + 25 * at, :]
-
-    def settle_rows(parts):
-        start, stop = CHUNKS[parts[0]][0], sum(CHUNKS[parts[-1]])
-        for end in range(2):
-            for part in parts:
-                if part > 0:
-                    circ(1 - end, part).wait_recv()
-            near[end, start:stop, :] = moved(recv[end, start:stop, :], swaps[end])
-
-    take_plane()
-
-    @pl.when(inner)
-    def _():
-        deliver().start()
-
-    settle_rows((0, 1, 2))
-    for end in range(2):
-        rows = slice(100 * end, 100 * end + 25)
-        order = (0, 1, 2, 3, 4, 5, 8)
-        own = [cells(src, rows) for src in order]
-        other = [None if src == 3 else far_value(end, src) for src in order]
-        left, right = (own, other) if end else (other, own)
-        sides[end] = left, right, reach_of(left, right)
-    settle((0, 1, 2, 4))
-    settle_rows((3,))
-    for end in range(2):
-        sides[end][1 if end else 0][3] = far_value(end, 3)
-    settle((3,))
+    settle_rows(far_end, (0, 1))
+    settle_rows(far_end, (2,))
+    reach = settle(far_end, (0, 1, 2, 4))
+    settle_rows(far_end, (3,))
+    settle(far_end, (3,), reach)
     @pl.when(jnp.logical_not(inner))
     def _():
         deliver().wait_recv()
@@ -583,6 +619,7 @@
     def values(pair):
         return [pair[f // 4][:, 32 * (f % 4) : 32 * (f % 4) + 32] for f in range(7)]
 
+    w = 0.5 * time_step * metric_scale[2] / end_weight
     diff, jump = face_parts(values(left), values(right), 2)
     sign = jnp.where(is_stator[:, :32], w, -w)
     fixes = jnp.concatenate([w * d + sign * j for d, j in zip(diff, jump)], axis=1)
@@ -595,28 +632,51 @@
         )
         add_axial(end, spread)
 
+    @pl.when(jnp.logical_not(is_first))
+    def _():
+        span_sent()
+
+    for end in range(2):
+        arrived_all(pack.at[end], circ_send.at[end])
+
+    @pl.when(inner)
+    def _():
+        deliver().wait_send()
+
+
+def update(partial_store, end_parts, fields, fields_next, store_next, ready, sent):
+    copies = []
     for f in range(5):
         for b in range(4):
-            rates[f, :, 128 * b : 128 * b + 128] = acc[f, b]
-    for end in range(2):
-        for part in range(len(CHUNKS)):
-            circ(end, part).wait_send()
-
-    @pl.when(inner)
-    def _():
-        deliver().wait_send()
+            cols = slice(128 * b, 128 * b + 128)
+            for start, stop, end in ((0, 25, 0), (25, 100, None), (100, 125, 1)):
+                rows = slice(start, stop)
+                value = partial_store[f, b, rows, :]
+                if end is not None:
+                    value = value + end_parts[end, f, 0:25, cols]
+                ready[1, f, rows, cols] = value
+                ready[0, f, rows, cols] = fields[f, rows, cols] + section_gain * value
+        for which, result in ((1, store_next), (0, fields_next)):
+            copies.append(pltpu.make_async_copy(ready.at[which, f], result.at[f], sent.at[which, f]))
+            copies[-1].start()
+    for copy in copies:
+        copy.wait()
 
 
 def on_device(mesh, radices, fields, section_store, mean_velocity, sound_speed, element_slot, face_turn, rotor_offset):
     nblk, nspan = mesh.shape["blk"], mesh.shape["span"]
     r0, r1, r2 = radices
     anywhere = pl.BlockSpec(memory_space=pltpu.HBM)
+    vmem = pl.BlockSpec(memory_space=pltpu.VMEM)
     dma = pltpu.SemaphoreType.DMA
-    rates = pl.pallas_call(
+    partial_store, end_parts = pl.pallas_call(
         functools.partial(kernel, radices, nblk, nspan),
-        out_shape=jax.ShapeDtypeStruct((5, 125, NB), F32),
-        in_specs=[anywhere] * 7,
-        out_specs=pl.BlockSpec(memory_space=pltpu.VMEM),
+        out_shape=(
+            jax.ShapeDtypeStruct((5, 4, 125, 128), F32),
+            jax.ShapeDtypeStruct((2, 5, 32, NB), F32),
+        ),
+        in_specs=[anywhere] * 8,
+        out_specs=(vmem, vmem),
         scratch_shapes=[
             pltpu.SMEM((1, 4), I32),
             pltpu.SMEM((4,), I32),
@@ -628,30 +688,32 @@
             pltpu.VMEM((2, PACK_ROWS, NB), F32),
             pltpu.VMEM((2, PACK_ROWS, NB), F32),
             pltpu.VMEM((2, PACK_ROWS, NB), F32),
+            pltpu.VMEM((2, NB, NB), BF16),
             pltpu.VMEM((4, 256, NB), F32),
             pltpu.VMEM((4, 256, NB), F32),
             pltpu.VMEM((4, 160, NB), F32),
-            pltpu.VMEM((2, 224, 128), F32),
-            pltpu.VMEM((2, 224, 128), F32),
+            pltpu.VMEM((2, PACK_ROWS, 128), F32),
+            pltpu.VMEM((2, 184, 128), F32),
             pltpu.VMEM((8, 256), F32),
             pltpu.VMEM((r0, 8, 256), F32),
             pltpu.VMEM((16, 256), F32),
             pltpu.VMEM((r1 * r2 - 1, 16, 256), F32),
             pltpu.VMEM((2, 8, 256), F32),
             pltpu.VMEM((8, 256), F32),
-            dma((10, 4)),
-            dma((2, len(CHUNKS))),
+            dma((13,)),
+            dma((5,)),
+            dma((2,)),
             dma((2, len(CHUNKS))),
             dma((2,)),
             dma((2,)),
             dma((r0,)),
             dma((r0,)),
-            dma((r1 * r2 - 1,)),
-            dma((r1 * r2 - 1,)),
+            dma((1,)),
+            dma((1,)),
             pltpu.SemaphoreType.REGULAR,
         ],
         compiler_params=pltpu.CompilerParams(
-            collective_id=0, has_side_effects=True, vmem_limit_bytes=40 * 2**20
+            collective_id=0, has_side_effects=True, vmem_limit_bytes=22 * 2**20
         ),
         name="rates",
     )(
@@ -659,6 +721,7 @@
             pltpu.with_memory_space_constraint(value, pltpu.HBM)
             for value in (
                 fields,
+                section_store,
                 mean_velocity,
                 sound_speed,
                 element_slot.reshape(1, NB),
@@ -668,8 +731,19 @@
             )
         ]
     )
-    store_next = section_decay * section_store + time_step * rates
-    fields_next = fields + section_gain * store_next
+    whole = jax.ShapeDtypeStruct((5, 125, NB), F32)
+    fields_next, store_next = pl.pallas_call(
+        update,
+        out_shape=(whole, whole),
+        in_specs=[vmem] * 3,
+        out_specs=(anywhere, anywhere),
+        scratch_shapes=[
+            pltpu.VMEM((2, 5, 125, NB), F32),
+            dma((2, 5)),
+        ],
+        compiler_params=pltpu.CompilerParams(vmem_limit_bytes=12 * 2**20),
+        name="update",
+    )(partial_store, end_parts, fields)
     return fields_next, store_next
 
 

time: 24.7 us -> 23.4 us (0.947)
  other arithmetic: 1.97 us -> 0 us
  Pallas kernels: 21.9 us -> 22.5 us
    add x1 -> x0, other arithmetic: 1.97 us -> none  [on_device(): fields_next = fields + section_gain * store_next]
    pallas_call x0 -> x1, Pallas kernels: none -> 1.65 us  [on_device(): pl.pallas_call(update, out_shape=(whole, whole), in_specs=[vmem] * 3, out...]
    pallas_call x1, Pallas kernels: 21.9 us -> 20.9 us  [on_device(): pl.pallas_call(functools.partial(kernel, radices, nblk, nspan), out_shape...]
where the time goes in v4:
time: 23.4 us; the launch traced here: 23.2 us
  Pallas kernels  22.5 us (96%)
  between operations  0.66 us (3%)
    pallas_call x1, Pallas kernels, on_device(): pl.pallas_call(functools.partial(kernel, radices, nblk, nspan), out_shape...  20.9 us
    pallas_call x1, Pallas kernels, on_device(): pl.pallas_call(update, out_shape=(whole, whole), in_specs=[vmem] * 3, out...  1.65 us

profile of v4, /device:TPU:0, one launch (start us, length us, event | category | flops | bytes accessed | tf_op | source)
XLA Modules:
  0.0 23.2 jit_solution(15961593579337819846)
XLA Ops:
  0.6 0.0 copy-start
  0.6 20.9 %rates.1 = (f32[5,4,125,128]{3,2,1,0:T(8,128)S(1)}, f32[2,5,32,512]{3,2,1,0:T(8,128)S(1)}) custom-call(f32[5,125,512]{2,1,0:T(8,128)} %fields.3, f32[5,125,512]{2,1,0:T(8,128)} %store.1, f32[3,125,512]{2,1,0:T(8,128)} %mean.1, f32[125,512]{1,0:T(8,128)} %sound.1, s32[1,512]{1,0:T(1,128)} %bitcast.1, bf16[2,3,125,125]{3,2,1,0:T(8,128)(2,1)} %constant.2.clone.slopes_hbm, ...), custom_call_target="tpu_custom_call" | custom-call | tf_op jit(solution)/shard_map/rates/pallas_call | solution.py:672
  21.5 0.0 copy-done
  21.5 1.6 %update.1 = (f32[5,125,512]{2,1,0:T(8,128)}, f32[5,125,512]{2,1,0:T(8,128)}) custom-call(f32[5,4,125,128]{3,2,1,0:T(8,128)S(1)} %get-tuple-element.4.partial_store, f32[2,5,32,512]{3,2,1,0:T(8,128)S(1)} %get-tuple-element.5.end_parts, f32[5,125,512]{2,1,0:T(8,128)S(1)} %copy-done), custom_call_target="tpu_custom_call" | custom-call | tf_op jit(solution)/shard_map/update/pallas_call | solution.py:735
Async XLA Ops:
  0.6 20.9 %copy-start = (f32[5,125,512]{2,1,0:T(8,128)S(1)}, f32[5,125,512]{2,1,0:T(8,128)}, u32[]{:S(2)}) copy-start(f32[5,125,512]{2,1,0:T(8,128)} %fields.3) | copy-start | bytes 3840004

commit v5 on v4

--- a/solution.py
+++ b/solution.py
@@ -92,19 +92,18 @@
 def turned(x, code, inverse):
     lane = lax.broadcasted_iota(I32, (8, 128), 1)
     n = lane & 31
-    i = (n * 13) >> 6
-    k = n - i * 5
+    row = (n * 13) >> 6
     ok = n < 25
-    base = lane - n
-
-    def apply(v, bit, target):
-        index = jnp.where(ok, base + target, lane)
-        return jnp.where((code & bit) != 0, jnp.take_along_axis(v, index, axis=1), v)
-
-    swap, first, second = (4, k * 5 + i), (1, (4 - i) * 5 + k), (2, i * 5 + 4 - k)
-    for bit, target in (second, first, swap) if inverse else (swap, first, second):
-        x = apply(x, bit, target)
-    return x
+    maps = {4: lambda i, k: (k, i), 1: lambda i, k: (4 - i, k), 2: lambda i, k: (i, 4 - k)}
+    result = x
+    for value in range(1, 8):
+        i, k = row, n - row * 5
+        for bit in (4, 1, 2) if inverse else (2, 1, 4):
+            if value & bit:
+                i, k = maps[bit](i, k)
+        index = jnp.where(ok, lane - n + i * 5 + k, lane)
+        result = jnp.where(code == value, jnp.take_along_axis(x, index, axis=1), result)
+    return result
 
 
 def kernel(
@@ -132,6 +131,7 @@
     recv,
     near,
     swaps,
+    hot_columns,
     face,
     grid,
     corr,
@@ -222,7 +222,7 @@
     for f in range(5):
         for b in range(4):
             pltpu.make_async_copy(
-                store.at[f, :, pl.ds(128 * b, 128)], old.at[f, b], old_sem.at[f]
+                store.at[f, :, pl.ds(128 * b, 128)], old.at[f, b], old_sem.at[0]
             ).start()
     load_turn.start()
     load_offset.start()
@@ -256,22 +256,31 @@
 
     every = range(len(CHUNKS))
 
-    for at, src in enumerate(PACK_ORDER):
-        loaded(src)
-        pack[1, 1 + 25 * at : 26 + 25 * at, :] = cells(src, slice(100, 125))
-
-    @pl.when(is_last)
-    def _():
-        pl.semaphore_wait(barrier, r0 + 1)
-        pl.semaphore_signal(far_sem, inc=1, device_id={"blk": after}, device_id_type=MESH)
-        for part in every:
-            circ(1, part).start()
-
     lane = lax.broadcasted_iota(I32, (8, NB), 1)
     sub = lax.broadcasted_iota(I32, (8, NB), 0)
     wanted = jnp.where(sub < 4, sub * 128 + (HALF - 1), (sub - 4) * 128 + HALF)
     column = jnp.sum(jnp.where(lane == wanted, slot_row, 0.0), axis=1, keepdims=True)
     hot = jnp.where(lane.astype(F32) == column, 1.0, 0.0)
+    wide = jnp.concatenate([hot, jnp.zeros((120, NB), F32)], axis=0)
+    hot_columns[...] = jnp.transpose(wide).astype(BF16)
+
+    def far_start(*parts):
+        @pl.when(is_last)
+        def _():
+            if parts[0] == 0:
+                pl.semaphore_wait(barrier, r0 + 1)
+                pl.semaphore_signal(far_sem, inc=1, device_id={"blk": after}, device_id_type=MESH)
+            for part in parts:
+                circ(1, part).start()
+
+    for at, src in enumerate(PACK_ORDER):
+        loaded(src)
+        pack[1, 1 + 25 * at : 26 + 25 * at, :] = cells(src, slice(100, 125))
+        if at == 1:
+            far_start(0)
+        if at == 3:
+            far_start(1)
+    far_start(2, 3)
 
     loaded(7)
     def pack_faces(d):
@@ -287,11 +296,13 @@
 
     pack_faces(2)
     dims = (((1,), (1,)), ((), ()))
-    packet = jnp.zeros((8, 256), F32)
-    for kind, rows in ((3, sub < 4), (2, sub >= 4)):
-        pick = jnp.where(rows, hot, 0.0).astype(BF16)
-        for part in halves(face[kind]):
-            packet = packet + lax.dot_general(pick, part, dims, preferred_element_type=F32)
+    picked = []
+    for kind in (3, 2):
+        both = jnp.concatenate(halves(face[kind]), axis=0)
+        part = jnp.dot(both, hot_columns[...], preferred_element_type=F32)
+        picked.append(part[:256] + part[256:])
+    stator_lane = lax.broadcasted_iota(I32, (256, 128), 1) < 4
+    packet = jnp.transpose(jnp.where(stator_lane, picked[0], picked[1]))[:8]
 
     sub1 = lax.broadcasted_iota(I32, (8, 128), 0)
     row = sub1 & 3
@@ -319,7 +330,7 @@
             src_ref=own_packet,
             dst_ref=gathered.at[from_z],
             send_sem=hop_send.at[to_z],
-            recv_sem=hop_recv.at[from_z],
+            recv_sem=hop_recv.at[0],
             device_id={"blk": t + to_z - z},
             device_id_type=MESH,
         )
@@ -345,11 +356,7 @@
     def take_collected():
         @pl.when(inner)
         def _():
-            for from_z in range(r0):
-
-                @pl.when(z != from_z)
-                def _():
-                    collect(1, from_z).wait_recv()
+            arrived_all(gathered.at[pl.ds(0, r0 - 1)], hop_recv.at[0])
 
         for to_z in range(1, r0 - 1):
 
@@ -436,13 +443,16 @@
 
     has_below, has_above = slab > 0, slab < nspan - 1
 
-    @pl.when(has_above)
-    def _():
-        span(1).start()
-
-    @pl.when(has_below)
-    def _():
-        span(0).start()
+    def start_span(when):
+        @pl.when(jnp.logical_and(when, has_above))
+        def _():
+            span(1).start()
+
+        @pl.when(jnp.logical_and(when, has_below))
+        def _():
+            span(0).start()
+
+    start_span(jnp.logical_not(is_last))
 
     for kind in (2, 3):
         grid[kind] = moved(face[kind], table[...])
@@ -459,8 +469,9 @@
     load_slopes.wait()
     velocity = (5, 6, 7)
 
+    arrived_all(old, old_sem.at[0])
+
     def volume(f):
-        arrived_all(old.at[f], old_sem.at[f])
         total = None
         for d in range(3):
             fx = cells(velocity[d]) * cells(f)
@@ -550,14 +561,11 @@
             fixed[end, f, 0:25, :] = sign * diff - weight0 * jump
         return reach
 
-    take_plane()
-
-    @pl.when(inner)
-    def _():
-        deliver().start()
-
-    settle_rows(near_end, (0, 1, 2, 3))
-    settle(near_end, (0, 1, 2, 3, 4))
+    @pl.when(is_last)
+    def _():
+        arrived_all(pack.at[1], circ_send.at[1])
+
+    start_span(is_last)
     @pl.when(has_above)
     def _():
         span(0).wait_recv()
@@ -598,46 +606,61 @@
                 for b in range(4):
                     part = back[32 * f + 5 * i : 32 * f + 5 * i + 5, 128 * b : 128 * b + 128]
                     acc[f, b, rows, :] += part
+    take_plane()
+
+    @pl.when(inner)
+    def _():
+        deliver().start()
+
+    settle_rows(near_end, (0, 1, 2, 3))
+    settle(near_end, (0, 1, 2, 3, 4))
     settle_rows(far_end, (0, 1))
+    def slide():
+        @pl.when(jnp.logical_not(inner))
+        def _():
+            deliver().wait_recv()
+
+        pair = []
+        for h in range(2):
+            lanes = slice(128 * h, 128 * h + 128)
+            pair.append(jnp.where(inner, final_out[0, :, lanes], final_in[:, lanes]))
+        pair = [jnp.where(is_stator, turned(p, code, False), p) for p in pair]
+        outer = [pltpu.roll(p, 4, axis=0) for p in pair]
+        left = [jnp.where(is_stator, a, b) for a, b in zip(own_pair, outer)]
+        right = [jnp.where(is_stator, b, a) for a, b in zip(own_pair, outer)]
+
+        def values(pair):
+            return [pair[f // 4][:, 32 * (f % 4) : 32 * (f % 4) + 32] for f in range(7)]
+
+        w = 0.5 * time_step * metric_scale[2] / end_weight
+        diff, jump = face_parts(values(left), values(right), 2)
+        sign = jnp.where(is_stator[:, :32], w, -w)
+        fixes = jnp.concatenate([w * d + sign * j for d, j in zip(diff, jump)], axis=1)
+        fixes = jnp.concatenate(halves(fixes), axis=0)
+        tn = (((0,), (0,)), ((), ()))
+        spots = jnp.concatenate([jnp.where(sub >= 4, hot, 0.0), jnp.where(sub < 4, hot, 0.0)], axis=1)
+        spots = jnp.concatenate([spots, spots], axis=0).astype(BF16)
+        spread = lax.dot_general(fixes, spots, tn, preferred_element_type=F32)
+        for end in range(2):
+            add_axial(end, spread[:, NB * end : NB * end + NB])
+
+    second = lax.rem(slab, 2) == 1
+    pl.when(second)(slide)
     settle_rows(far_end, (2,))
     reach = settle(far_end, (0, 1, 2, 4))
     settle_rows(far_end, (3,))
     settle(far_end, (3,), reach)
-    @pl.when(jnp.logical_not(inner))
-    def _():
-        deliver().wait_recv()
-
-    pair = []
-    for h in range(2):
-        lanes = slice(128 * h, 128 * h + 128)
-        pair.append(jnp.where(inner, final_out[0, :, lanes], final_in[:, lanes]))
-    pair = [jnp.where(is_stator, turned(p, code, False), p) for p in pair]
-    outer = [pltpu.roll(p, 4, axis=0) for p in pair]
-    left = [jnp.where(is_stator, a, b) for a, b in zip(own_pair, outer)]
-    right = [jnp.where(is_stator, b, a) for a, b in zip(own_pair, outer)]
-
-    def values(pair):
-        return [pair[f // 4][:, 32 * (f % 4) : 32 * (f % 4) + 32] for f in range(7)]
-
-    w = 0.5 * time_step * metric_scale[2] / end_weight
-    diff, jump = face_parts(values(left), values(right), 2)
-    sign = jnp.where(is_stator[:, :32], w, -w)
-    fixes = jnp.concatenate([w * d + sign * j for d, j in zip(diff, jump)], axis=1)
-    fixes = jnp.concatenate(halves(fixes), axis=0)
-    tn = (((0,), (0,)), ((), ()))
-    for end in range(2):
-        mine = jnp.where(sub < 4 if end else sub >= 4, hot, 0.0).astype(BF16)
-        spread = lax.dot_general(
-            fixes, jnp.concatenate([mine, mine], axis=0), tn, preferred_element_type=F32
-        )
-        add_axial(end, spread)
-
+    pl.when(jnp.logical_not(second))(slide)
     @pl.when(jnp.logical_not(is_first))
     def _():
         span_sent()
 
-    for end in range(2):
-        arrived_all(pack.at[end], circ_send.at[end])
+    arrived_all(pack.at[0], circ_send.at[0])
+
+    @pl.when(jnp.logical_not(is_last))
+    def _():
+        arrived_all(pack.at[1], circ_send.at[1])
+
 
     @pl.when(inner)
     def _():
@@ -689,6 +712,7 @@
             pltpu.VMEM((2, PACK_ROWS, NB), F32),
             pltpu.VMEM((2, PACK_ROWS, NB), F32),
             pltpu.VMEM((2, NB, NB), BF16),
+            pltpu.VMEM((NB, 128), BF16),
             pltpu.VMEM((4, 256, NB), F32),
             pltpu.VMEM((4, 256, NB), F32),
             pltpu.VMEM((4, 160, NB), F32),
@@ -701,13 +725,13 @@
             pltpu.VMEM((2, 8, 256), F32),
             pltpu.VMEM((8, 256), F32),
             dma((13,)),
-            dma((5,)),
+            dma((1,)),
             dma((2,)),
             dma((2, len(CHUNKS))),
             dma((2,)),
             dma((2,)),
             dma((r0,)),
-            dma((r0,)),
+            dma((1,)),
             dma((1,)),
             dma((1,)),
             pltpu.SemaphoreType.REGULAR,

time: 23.4 us -> 22.7 us (0.970)
  Pallas kernels: 22.5 us -> 22 us
    pallas_call x1, Pallas kernels: 20.9 us -> 20.3 us  [on_device(): pl.pallas_call(functools.partial(kernel, radices, nblk, nspan), out_shape...]
where the time goes in v5:
time: 22.7 us; the launch traced here: 22.6 us
  Pallas kernels  22 us (97%)
  between operations  0.66 us (3%)
    pallas_call x1, Pallas kernels, on_device(): pl.pallas_call(functools.partial(kernel, radices, nblk, nspan), out_shape...  20.3 us
    pallas_call x1, Pallas kernels, on_device(): pl.pallas_call(update, out_shape=(whole, whole), in_specs=[vmem] * 3, out...  1.65 us

profile of v5, /device:TPU:0, one launch (start us, length us, event | category | flops | bytes accessed | tf_op | source)
XLA Modules:
  0.0 22.6 jit_solution(14781586556943846788)
XLA Ops:
  0.6 0.0 copy-start
  0.6 20.3 %rates.1 = (f32[5,4,125,128]{3,2,1,0:T(8,128)S(1)}, f32[2,5,32,512]{3,2,1,0:T(8,128)S(1)}) custom-call(f32[5,125,512]{2,1,0:T(8,128)} %fields.3, f32[5,125,512]{2,1,0:T(8,128)} %store.1, f32[3,125,512]{2,1,0:T(8,128)} %mean.1, f32[125,512]{1,0:T(8,128)} %sound.1, s32[1,512]{1,0:T(1,128)} %bitcast.1, bf16[2,3,125,125]{3,2,1,0:T(8,128)(2,1)} %constant.2.clone.slopes_hbm, ...), custom_call_target="tpu_custom_call" | custom-call | tf_op jit(solution)/shard_map/rates/pallas_call | solution.py:695
  21.0 0.0 copy-done
  21.0 1.6 %update.1 = (f32[5,125,512]{2,1,0:T(8,128)}, f32[5,125,512]{2,1,0:T(8,128)}) custom-call(f32[5,4,125,128]{3,2,1,0:T(8,128)S(1)} %get-tuple-element.4.partial_store, f32[2,5,32,512]{3,2,1,0:T(8,128)S(1)} %get-tuple-element.5.end_parts, f32[5,125,512]{2,1,0:T(8,128)S(1)} %copy-done), custom_call_target="tpu_custom_call" | custom-call | tf_op jit(solution)/shard_map/update/pallas_call | solution.py:759
Async XLA Ops:
  0.6 20.3 %copy-start = (f32[5,125,512]{2,1,0:T(8,128)S(1)}, f32[5,125,512]{2,1,0:T(8,128)}, u32[]{:S(2)}) copy-start(f32[5,125,512]{2,1,0:T(8,128)} %fields.3) | copy-start | bytes 3840004

commit v6 on v5

--- a/solution.py
+++ b/solution.py
@@ -120,6 +120,7 @@
     offset_hbm,
     acc,
     fixed,
+    held,
     turn,
     offset,
     x,
@@ -173,23 +174,8 @@
                 to = z + r0 * lax.rem(y + dy, r1) + r0 * r1 * lax.rem(x_at + dx, r2)
                 plane.append((dy, dx, to))
 
-    barrier = pltpu.get_barrier_semaphore()
-    for to in (above, below):
-        pl.semaphore_signal(barrier, inc=1, device_id={"span": to}, device_id_type=MESH)
-    for to, skip in zip(run, across):
-
-        @pl.when(jnp.logical_not(skip))
-        def _():
-            pl.semaphore_signal(barrier, inc=1, device_id={"blk": to}, device_id_type=MESH)
-
-    @pl.when(inner)
-    def _():
-        for _, _, to in plane:
-            pl.semaphore_signal(barrier, inc=1, device_id={"blk": to}, device_id_type=MESH)
-
-    @pl.when(is_first)
-    def _():
-        pl.semaphore_signal(barrier, inc=1, device_id={"blk": before}, device_id_type=MESH)
+    def place(src):
+        return held.at[src] if src < 5 else x.at[src - 5]
 
     def load(src):
         if src < 5:
@@ -197,7 +183,7 @@
         else:
             array = mean.at[src - 5] if src < 8 else sound
         return [
-            pltpu.make_async_copy(array.at[:, pl.ds(128 * b, 128)], x.at[src, b], load_sem.at[src])
+            pltpu.make_async_copy(array.at[:, pl.ds(128 * b, 128)], place(src).at[b], load_sem.at[src])
             for b in range(4)
         ]
 
@@ -205,17 +191,39 @@
         pltpu.make_async_copy(ref, ref, sem).wait()
 
     def loaded(src):
-        arrived_all(x.at[src], load_sem.at[src])
+        arrived_all(place(src), load_sem.at[src])
 
     def cells(src, rows=slice(0, 125)):
-        return jnp.concatenate([x[src, b, rows, :] for b in range(4)], axis=1)
+        return jnp.concatenate([place(src)[b, rows, :] for b in range(4)], axis=1)
 
     load_slot = pltpu.make_async_copy(slot_hbm, slot, load_sem.at[9])
     load_slopes = pltpu.make_async_copy(slopes_hbm, slopes, load_sem.at[10])
     load_turn = pltpu.make_async_copy(turn_hbm, turn, load_sem.at[11])
     load_offset = pltpu.make_async_copy(offset_hbm, offset, load_sem.at[12])
     load_slot.start()
-    for src in PACK_ORDER + (7, 6):
+    for src in PACK_ORDER[:2]:
+        for copy in load(src):
+            copy.start()
+
+    barrier = pltpu.get_barrier_semaphore()
+    for to in (above, below):
+        pl.semaphore_signal(barrier, inc=1, device_id={"span": to}, device_id_type=MESH)
+    for to, skip in zip(run, across):
+
+        @pl.when(jnp.logical_not(skip))
+        def _():
+            pl.semaphore_signal(barrier, inc=1, device_id={"blk": to}, device_id_type=MESH)
+
+    @pl.when(inner)
+    def _():
+        for _, _, to in plane:
+            pl.semaphore_signal(barrier, inc=1, device_id={"blk": to}, device_id_type=MESH)
+
+    @pl.when(is_first)
+    def _():
+        pl.semaphore_signal(barrier, inc=1, device_id={"blk": before}, device_id_type=MESH)
+
+    for src in PACK_ORDER[2:] + (7, 6):
         for copy in load(src):
             copy.start()
     load_slopes.start()
@@ -256,6 +264,29 @@
 
     every = range(len(CHUNKS))
 
+    def far_start(*parts):
+        @pl.when(is_last)
+        def _():
+            if parts[0] == 0:
+                pl.semaphore_wait(barrier, r0 + 1)
+                pl.semaphore_signal(far_sem, inc=1, device_id={"blk": after}, device_id_type=MESH)
+            for part in parts:
+                circ(1, part).start()
+
+    def pack_high(at):
+        pack[1, 1 + 25 * at : 26 + 25 * at, :] = cells(PACK_ORDER[at], slice(100, 125))
+
+    loaded(5)
+    pack_high(0)
+    loaded(8)
+    pack_high(1)
+    far_start(0)
+    loaded(1)
+    pack_high(2)
+    loaded(4)
+    pack_high(3)
+    far_start(1)
+
     lane = lax.broadcasted_iota(I32, (8, NB), 1)
     sub = lax.broadcasted_iota(I32, (8, NB), 0)
     wanted = jnp.where(sub < 4, sub * 128 + (HALF - 1), (sub - 4) * 128 + HALF)
@@ -264,25 +295,8 @@
     wide = jnp.concatenate([hot, jnp.zeros((120, NB), F32)], axis=0)
     hot_columns[...] = jnp.transpose(wide).astype(BF16)
 
-    def far_start(*parts):
-        @pl.when(is_last)
-        def _():
-            if parts[0] == 0:
-                pl.semaphore_wait(barrier, r0 + 1)
-                pl.semaphore_signal(far_sem, inc=1, device_id={"blk": after}, device_id_type=MESH)
-            for part in parts:
-                circ(1, part).start()
-
-    for at, src in enumerate(PACK_ORDER):
+    for src in PACK_ORDER[4:] + (7,):
         loaded(src)
-        pack[1, 1 + 25 * at : 26 + 25 * at, :] = cells(src, slice(100, 125))
-        if at == 1:
-            far_start(0)
-        if at == 3:
-            far_start(1)
-    far_start(2, 3)
-
-    loaded(7)
     def pack_faces(d):
         for at, src in enumerate((0, 1, 2, 3, 4, 4 + 1 + d, 8)):
             for end in range(2):
@@ -345,6 +359,9 @@
         def _():
             collect(to_z, z).start()
 
+    for at in (4, 5, 6):
+        pack_high(at)
+    far_start(2, 3)
     for at, src in enumerate(PACK_ORDER):
         pack[0, 1 + 25 * at : 26 + 25 * at, :] = cells(src, slice(0, 25))
     start_circ(*every)
@@ -648,9 +665,9 @@
     pl.when(second)(slide)
     settle_rows(far_end, (2,))
     reach = settle(far_end, (0, 1, 2, 4))
+    pl.when(jnp.logical_not(second))(slide)
     settle_rows(far_end, (3,))
     settle(far_end, (3,), reach)
-    pl.when(jnp.logical_not(second))(slide)
     @pl.when(jnp.logical_not(is_first))
     def _():
         span_sent()
@@ -678,7 +695,7 @@
                 if end is not None:
                     value = value + end_parts[end, f, 0:25, cols]
                 ready[1, f, rows, cols] = value
-                ready[0, f, rows, cols] = fields[f, rows, cols] + section_gain * value
+                ready[0, f, rows, cols] = fields[f, b, rows, :] + section_gain * value
         for which, result in ((1, store_next), (0, fields_next)):
             copies.append(pltpu.make_async_copy(ready.at[which, f], result.at[f], sent.at[which, f]))
             copies[-1].start()
@@ -692,18 +709,19 @@
     anywhere = pl.BlockSpec(memory_space=pltpu.HBM)
     vmem = pl.BlockSpec(memory_space=pltpu.VMEM)
     dma = pltpu.SemaphoreType.DMA
-    partial_store, end_parts = pl.pallas_call(
+    partial_store, end_parts, held_fields = pl.pallas_call(
         functools.partial(kernel, radices, nblk, nspan),
         out_shape=(
             jax.ShapeDtypeStruct((5, 4, 125, 128), F32),
             jax.ShapeDtypeStruct((2, 5, 32, NB), F32),
+            jax.ShapeDtypeStruct((5, 4, 125, 128), F32),
         ),
         in_specs=[anywhere] * 8,
-        out_specs=(vmem, vmem),
+        out_specs=(vmem, vmem, vmem),
         scratch_shapes=[
             pltpu.SMEM((1, 4), I32),
             pltpu.SMEM((4,), I32),
-            pltpu.VMEM((9, 4, 125, 128), F32),
+            pltpu.VMEM((4, 4, 125, 128), F32),
             pltpu.VMEM((5, 4, 125, 128), F32),
             pltpu.VMEM((1, NB), I32),
             pltpu.VMEM((2, 3, 125, 125), BF16),
@@ -767,7 +785,7 @@
         ],
         compiler_params=pltpu.CompilerParams(vmem_limit_bytes=12 * 2**20),
         name="update",
-    )(partial_store, end_parts, fields)
+    )(partial_store, end_parts, held_fields)
     return fields_next, store_next
 
 

time: 22.7 us -> 22.7 us (level)
  no operation moved by 1% of the time
where the time goes in v6:
time: 22.7 us; the launch traced here: 22.5 us
  Pallas kernels  21.8 us (96%)
  between operations  0.64 us (3%)
    pallas_call x1, Pallas kernels, on_device(): pl.pallas_call(functools.partial(kernel, radices, nblk, nspan), out_shape...  20.2 us
    pallas_call x1, Pallas kernels, on_device(): pl.pallas_call(update, out_shape=(whole, whole), in_specs=[vmem] * 3, out...  1.64 us

profile of v6, /device:TPU:0, one launch (start us, length us, event | category | flops | bytes accessed | tf_op | source)
XLA Modules:
  0.0 22.5 jit_solution(1810181531891756522)
XLA Ops:
  0.6 20.2 %rates.1 = (f32[5,4,125,128]{3,2,1,0:T(8,128)S(1)}, f32[2,5,32,512]{3,2,1,0:T(8,128)S(1)}, f32[5,4,125,128]{3,2,1,0:T(8,128)S(1)}) custom-call(f32[5,125,512]{2,1,0:T(8,128)} %fields.1, f32[5,125,512]{2,1,0:T(8,128)} %store.1, f32[3,125,512]{2,1,0:T(8,128)} %mean.1, f32[125,512]{1,0:T(8,128)} %sound.1, s32[1,512]{1,0:T(1,128)} %bitcast.1, ...), custom_call_target="tpu_custom_call" | custom-call | tf_op jit(solution)/shard_map/rates/pallas_call | solution.py:712
  20.8 1.6 %update.1 = (f32[5,125,512]{2,1,0:T(8,128)}, f32[5,125,512]{2,1,0:T(8,128)}) custom-call(f32[5,4,125,128]{3,2,1,0:T(8,128)S(1)} %get-tuple-element.5.partial_store, f32[2,5,32,512]{3,2,1,0:T(8,128)S(1)} %get-tuple-element.6.end_parts, f32[5,4,125,128]{3,2,1,0:T(8,128)S(1)} %get-tuple-element.7.fields), custom_call_target="tpu_custom_call" | custom-call | tf_op jit(solution)/shard_map/update/pallas_call | solution.py:777
